TPU v7x, 8 devices: a whole 2x2x1 slice. The times are simulated.
8 devices in a mesh: data: 8 (over z, y, x, core).
Axes of the slice: x: 2, y: 2, z: 1, core: 2. Of those that a mesh axis runs over, the one named last changes fastest.
Arguments:
- w_in: float32 [8, 1024, 4096], replicated
- w_out: float32 [8, 4096, 1024], replicated
- mom_in: float32 [8, 1024, 4096], replicated
- mom_out: float32 [8, 4096, 1024], replicated
- x_first: bfloat16 [8192, 1024], P('data')
- y_first: bfloat16 [8192, 1024], P('data')
- x_second: bfloat16 [8192, 1024], P('data')
- y_second: bfloat16 [8192, 1024], P('data')
Outputs:
- output 1: float32 [8, 1024, 4096], replicated
- output 2: float32 [8, 4096, 1024], replicated
- output 3: float32 [8, 1024, 4096], replicated
- output 4: float32 [8, 4096, 1024], replicated
- output 5: float32 [8192], P('data')
- output 6: float32 [8192, 1024], P('data')
All inputs are finite; a program needn't handle non-finite values.
Results may differ from a plain program's by a relative error of at most 0.00755736.
Values are sent between devices in bfloat16 or wider.
A program may use at most 4.25 GiB of HBM per device.

v0:
```python
import jax
import jax.numpy as jnp
from jax import lax
from jax.sharding import PartitionSpec as P

LR_SCALE = 1.0
MOMENTUM = 0.9
ROW_CONTRACT = (((0,), (0,)), ((), ()))
COL_CONTRACT = (((1,), (1,)), ((), ()))


def forward_stack(w_in_list, w_out_list, h_cur):
    saved_acts = []
    for w_in_l, w_out_l in zip(w_in_list, w_out_list):
        h_bf = h_cur.astype(jnp.bfloat16)
        pre_act = jnp.dot(h_bf, w_in_l, preferred_element_type=jnp.float32)
        act_bf = jax.nn.gelu(pre_act).astype(jnp.bfloat16)
        h_cur = h_cur + jnp.dot(act_bf, w_out_l, preferred_element_type=jnp.float32)
        saved_acts.append((h_bf, pre_act, act_bf))
    return h_cur, saved_acts


def layer_backward(w_in_l, w_out_l, saved_layer, err_row, need_err):
    h_bf, pre_act, act_bf = saved_layer
    err_bf = err_row.astype(jnp.bfloat16)
    grad_out = lax.dot_general(act_bf, err_bf, ROW_CONTRACT, preferred_element_type=jnp.float32)
    d_act = lax.dot_general(err_bf, w_out_l, COL_CONTRACT, preferred_element_type=jnp.float32)
    d_pre = jax.vjp(jax.nn.gelu, pre_act)[1](d_act)[0].astype(jnp.bfloat16)
    grad_in = lax.dot_general(h_bf, d_pre, ROW_CONTRACT, preferred_element_type=jnp.float32)
    if need_err:
        err_row = err_row + lax.dot_general(d_pre, w_in_l, COL_CONTRACT, preferred_element_type=jnp.float32)
    return grad_in.astype(jnp.bfloat16), grad_out.astype(jnp.bfloat16), err_row


def apply_update(weights, moments, grad_sum, step_size):
    mom_new = MOMENTUM * moments + grad_sum.astype(jnp.float32)
    return weights - step_size * mom_new, mom_new


def solution(mesh):
    groups = mesh.shape["data"]
    rows_spec = P("data", None)

    def local_steps(w_in, w_out, mom_in, mom_out, x_first, y_first, x_second, y_second):
        layers = w_in.shape[0]
        tok_local, model_dim = x_first.shape
        step_size = LR_SCALE / layers
        w_in_list = [w_in[layer_idx].astype(jnp.bfloat16) for layer_idx in range(layers)]
        w_out_list = [w_out[layer_idx].astype(jnp.bfloat16) for layer_idx in range(layers)]
        h_last, saved_acts = forward_stack(w_in_list, w_out_list, x_first.astype(jnp.float32))
        err_row = (h_last - y_first.astype(jnp.float32)) * (1.0 / (tok_local * groups * model_dim))
        sums_in = [None] * layers
        sums_out = [None] * layers
        for layer_idx in reversed(range(layers)):
            grad_in, grad_out, err_row = layer_backward(w_in_list[layer_idx], w_out_list[layer_idx], saved_acts[layer_idx], err_row, layer_idx > 0)
            sums_in[layer_idx], sums_out[layer_idx] = lax.psum((grad_in, grad_out), "data")
        w_in_new, mom_in_new = apply_update(w_in, mom_in, jnp.stack(sums_in), step_size)
        w_out_new, mom_out_new = apply_update(w_out, mom_out, jnp.stack(sums_out), step_size)
        new_in_list = [w_in_new[layer_idx].astype(jnp.bfloat16) for layer_idx in range(layers)]
        new_out_list = [w_out_new[layer_idx].astype(jnp.bfloat16) for layer_idx in range(layers)]
        h_next, unused = forward_stack(new_in_list, new_out_list, x_second.astype(jnp.float32))
        row_diff = h_next - y_second.astype(jnp.float32)
        loss_rows = jnp.sum(row_diff * row_diff, axis=-1) / (2 * model_dim)
        return w_in_new, w_out_new, mom_in_new, mom_out_new, loss_rows, h_next

    return jax.shard_map(local_steps, mesh=mesh, in_specs=(P(), P(), P(), P(), rows_spec, rows_spec, rows_spec, rows_spec), out_specs=(P(), P(), P(), P(), P("data"), rows_spec), check_vma=False)
```

profile of v0, /device:TPU:0, one launch (start us, length us, event | category | flops | bytes accessed | tf_op | source)
XLA Modules:
  0.0 3435.1 jit_solution(13066760825869842577)
XLA Ops:
  7.2 63.6 %convert.40 = bf16[8,1024,4096]{2,1,0:T(8,128)(2,1)} convert(f32[8,1024,4096]{2,1,0:T(8,128)} %param.8) | non-fusion elementwise | flops 33554432 | bytes 201326592 | tf_op jit(solution)/shard_map/convert.31
  70.8 63.8 %convert.41 = bf16[8,4096,1024]{2,1,0:T(8,128)(2,1)} convert(f32[8,4096,1024]{2,1,0:T(8,128)} %param.9) | non-fusion elementwise | flops 33554432 | bytes 201326592 | tf_op jit(solution)/shard_map/convert.30
  396.9 25.4 fusion.55
  438.7 17.7 convert_bitcast_fusion.1
  456.4 25.3 fusion.48
  515.5 25.2 fusion.41
  557.1 17.6 convert_bitcast_fusion.3
  574.7 25.3 fusion.34
  633.8 25.3 fusion.27
  693.1 25.3 fusion.20
  752.2 25.3 fusion.13
  912.3 30.5 convert_bitcast_fusion.15
  942.9 18.5 convert_bitcast_fusion
  961.4 121.5 %copy.22 = f32[8,1024,4096]{1,2,0:T(8,128)} copy(f32[8,1024,4096]{2,1,0:T(8,128)} %param.8) | data formatting | bytes 268435456 | tf_op args[0]
  1083.0 121.7 %copy.14 = f32[8,1024,4096]{1,2,0:T(8,128)} copy(f32[8,1024,4096]{2,1,0:T(8,128)} %param.10) | data formatting | bytes 268435456 | tf_op args[2]
  1211.3 1109.7 %all-reduce.6.cloned.1.call-done = (bf16[1,1024,4096]{1,2,0:T(8,128)(2,1)}, bf16[1,1024,4096]{1,2,0:T(8,128)(2,1)}, bf16[1,1024,4096]{1,2,0:T(8,128)(2,1)}, bf16...) async-done(((bf16[1,1024,4096]{1,2,0:T(8,128)(2,1)}, ...) | async-done | bytes 125829136 | tf_op jit(solution)/shard_map/psum | solution.py:56
  2381.9 58.2 %all-reduce.4.cloned.1.call-done = bf16[1,4096,1024]{2,1,0:T(8,128)(2,1)} async-done(((bf16[1,4096,1024]{2,1,0:T(8,128)(2,1)}), bf16[1,4096,1024]{2,1,0:T(8,128)(2,1)}) %all-reduce.4.cloned.1.call-update) | async-done | bytes 8388624 | tf_op jit(solution)/shard_map/psum | solution.py:56
  2447.7 212.0 %fusion.315 = (bf16[8,4096,1024]{2,1,0:T(8,128)(2,1)}, f32[8,4096,1024]{2,1,0:T(8,128)}, f32[8,4096,1024]{2,1,0:T(8,128)}) fusion(f32[8,4096,1024]{2,1,0:T(8,128)} %param.9, bf16[8,4096,1024]{2,1,0:T(8,128)(2,1)} %constant_dynamic-update-slice_fusion.8, f32[8,4096,1024]{2,1,0:T(8,128)} %param.11), kind=kLoop, calls=%fused_computation.390 | loop fusion | flops 201326592 | bytes 671088640 | tf_op jit(solution)/shard_map/convert.14
  2713.1 212.3 %fusion.314 = (bf16[8,1024,4096]{1,2,0:T(8,128)(2,1)}, f32[8,1024,4096]{1,2,0:T(8,128)}, f32[8,1024,4096]{1,2,0:T(8,128)}) fusion(f32[8,1024,4096]{1,2,0:T(8,128)} %copy.22, bf16[8,1024,4096]{1,2,0:T(8,128)(2,1)} %constant_dynamic-update-slice_fusion, f32[8,1024,4096]{1,2,0:T(8,128)} %copy.14), kind=kLoop, calls=%fused_computation.389 | loop fusion | flops 201326592 | bytes 671088640 | tf_op jit(solution)/shard_map/convert.15
  2925.5 24.1 fusion.120
  2949.5 29.6 fusion.204
  3161.4 17.8 multiply_reduce_fusion
  3185.1 121.4 %copy.26 = f32[8,1024,4096]{2,1,0:T(8,128)} copy(f32[8,1024,4096]{1,2,0:T(8,128)} %get-tuple-element.28) | data formatting | bytes 268435456
  3306.4 121.4 %copy.27 = f32[8,1024,4096]{2,1,0:T(8,128)} copy(f32[8,1024,4096]{1,2,0:T(8,128)} %get-tuple-element.29) | data formatting | bytes 268435456
  (126 shorter events, 881.9 us)
Async XLA Ops:
  7.2 2313.9 %all-reduce.6.cloned.1.call-start = ((), (), s32[]{:S(2)}) async-start(), calls=%async_computation.1 | async-start | bytes 251658240 | tf_op jit(solution)/shard_map/psum | solution.py:56
  70.8 63.8 %copy-start.4 = (bf16[1024,1024]{1,0:T(8,128)(2,1)S(1)}, bf16[1024,1024]{1,0:T(8,128)(2,1)}, u32[]{:S(2)}) copy-start(bf16[1024,1024]{1,0:T(8,128)(2,1)} %param.12) | copy-start | bytes 6291460
  165.2 2.0 copy-start.14
  198.8 16.0 copy-start.6
  232.3 16.9 copy-start.8
  265.4 16.0 copy-start.9
  297.7 16.1 copy-start.10
  329.9 16.1 copy-start.11
  363.5 15.9 copy-start.3
  363.5 15.9 copy-start.13
  436.7 2.0 copy-start.21
  777.4 15.0 copy-start.12
  777.4 29.8 slice-start
  792.4 14.9 slice-start.1
  807.3 28.9 slice-start.2
  821.4 14.7 slice-start.3
  836.1 13.6 copy-start.7
  849.8 15.0 copy-start.16
  864.8 13.9 copy-start.5
  878.7 16.2 copy-start.22
  942.9 1497.2 %all-reduce.4.cloned.1.call-start = ((), (), s32[]{:S(2)}) async-start(), calls=%async_computation | async-start | bytes 16777216 | tf_op jit(solution)/shard_map/psum | solution.py:56
  1083.0 125.6 %copy-start = (bf16[1024,1024]{1,0:T(8,128)(2,1)S(1)}, bf16[1024,1024]{1,0:T(8,128)(2,1)}, u32[]{:S(2)}) copy-start(bf16[1024,1024]{1,0:T(8,128)(2,1)} %param.15) | copy-start | bytes 6291460
  2713.1 212.3 %copy-start.1 = (bf16[1024,1024]{1,0:T(8,128)(2,1)S(1)}, bf16[1024,1024]{1,0:T(8,128)(2,1)}, u32[]{:S(2)}) copy-start(bf16[1024,1024]{1,0:T(8,128)(2,1)} %param.14) | copy-start | bytes 6291460
  3145.2 16.1 copy-start.2
  (5 other events, 9.9 us)
Sparse Core Ops, SparseCore 0:
  943.0 1377.9 all-reduce.5
  2325.0 114.9 all-reduce.3
where the time goes:
time: 3450 us; the launch traced here: 3440 us
  waiting for transfers between devices  1170 us (34%)
  matrix products  1070 us (31%)
  local copies, waits for them, and re-layouts  634 us (18%)
  other arithmetic  552 us (16%)
    psum x2, waiting for transfers between devices, local_steps(): lax.psum((grad_in, grad_out), 'data')  1170 us
    unnamed x75, local copies, waits for them, and re-layouts  619 us
    another operation x4, other arithmetic  552 us
    dot_general x16, matrix products, forward_stack(): h_cur = h_cur + jnp.dot(act_bf, w_out_l, preferred_element_type=jnp.float32)  292 us
    dot_general x14, matrix products, forward_stack(): pre_act = jnp.dot(h_bf, w_in_l, preferred_element_type=jnp.float32)  222 us
    dot_general x7, matrix products, layer_backward(): lax.dot_general(err_bf, w_out_l, COL_CONTRACT, preferred_element_type=jnp...  177 us
    dot_general x8, matrix products, layer_backward(): lax.dot_general(act_bf, err_bf, ROW_CONTRACT, preferred_element_type=jnp....  141 us
    dot_general x8, matrix products, layer_backward(): lax.dot_general(h_bf, d_pre, ROW_CONTRACT, preferred_element_type=jnp.flo...  134 us
  transfers between devices with their start and end apart: 2, of which 2 were waited for; matrix products, arithmetic and copies ran while one was open for 10% of the time, Pallas kernels for 0%

commit v1 on v0

v1 whole, which is shorter than its diff:
```python
import functools
import math

import jax
import jax.numpy as jnp
from jax import lax
from jax.experimental import pallas as pl
from jax.experimental.pallas import tpu as pltpu
from jax.sharding import PartitionSpec as P


LR_SCALE = 1.0
MOMENTUM = 0.9
GELU_C = math.sqrt(2.0 / math.pi)
GELU_K = 0.044715
BF = jnp.bfloat16
F32 = jnp.float32
ROWS_BOTH = (((0,), (0,)), ((), ()))
COLS_BOTH = (((1,), (1,)), ((), ()))
PLAIN = (((1,), (0,)), ((), ()))
VMEM_LIMIT = 60 * 1024 * 1024


def dot(a, b, dims=PLAIN):
    return lax.dot_general(a, b, dims, preferred_element_type=F32)


def gelu_tanh(z):
    return jnp.tanh(GELU_C * (z + GELU_K * (z * z * z)))


def gelu(z):
    return z * (0.5 * (1.0 + gelu_tanh(z)))


def cost(flops, nbytes):
    return pl.CostEstimate(flops=int(flops), bytes_accessed=int(nbytes), transcendentals=0)


def forward_body(err_scale, chunk, x_ref, y_ref, w1_ref, w2_ref, z_ref, hb_ref, e_ref, h_scr, hb_scr):
    layer, tile = pl.program_id(0), pl.program_id(1)

    @pl.when((layer == 0) & (tile == 0))
    def _():
        h_scr[...] = x_ref[...].astype(F32)

    @pl.when(tile == 0)
    def _():
        hb = h_scr[...].astype(BF)
        hb_scr[...] = hb
        hb_ref[0] = hb

    w1 = w1_ref[0].astype(BF)
    w2 = w2_ref[0].astype(BF)
    rows = h_scr.shape[0]
    for start in range(0, rows, chunk):
        z = dot(hb_scr[start : start + chunk, :], w1)
        z_ref[0, start : start + chunk, :] = z
        h_scr[start : start + chunk, :] += dot(gelu(z).astype(BF), w2)

    @pl.when((layer == pl.num_programs(0) - 1) & (tile == pl.num_programs(1) - 1))
    def _():
        e_ref[...] = (h_scr[...] - y_ref[...].astype(F32)) * err_scale


def forward_first(x, y, w_in, w_out, err_scale, tile=512, chunk=256):
    layers, dim, hidden = w_in.shape
    rows = x.shape[0]
    whole = pl.BlockSpec((rows, dim), lambda l, j: (0, 0))
    return pl.pallas_call(
        functools.partial(forward_body, err_scale, chunk),
        grid=(layers, hidden // tile),
        in_specs=[
            whole,
            whole,
            pl.BlockSpec((1, dim, tile), lambda l, j: (l, 0, j)),
            pl.BlockSpec((1, tile, dim), lambda l, j: (l, j, 0)),
        ],
        out_specs=[
            pl.BlockSpec((1, rows, tile), lambda l, j: (l, 0, j)),
            pl.BlockSpec((1, rows, dim), lambda l, j: (l, 0, 0)),
            whole,
        ],
        out_shape=[
            jax.ShapeDtypeStruct((layers, rows, hidden), F32),
            jax.ShapeDtypeStruct((layers, rows, dim), BF),
            jax.ShapeDtypeStruct((rows, dim), F32),
        ],
        scratch_shapes=[pltpu.VMEM((rows, dim), F32), pltpu.VMEM((rows, dim), BF)],
        compiler_params=pltpu.CompilerParams(
            dimension_semantics=("arbitrary", "arbitrary"), vmem_limit_bytes=VMEM_LIMIT
        ),
        cost_estimate=cost(4 * layers * rows * dim * hidden, layers * (8 * dim * hidden + 4 * rows * hidden)),
        name="forward_first",
    )(x, y, w_in, w_out)


def backward_body(blocks, chunk, layer_ref, e_ref, hb_ref, w1_ref, w2_ref, z_ref, g_hbm, e_out, eb_scr, a_scr, s_scr, g1_scr, g2_scr, sems):
    tile_id = pl.program_id(0)
    slot = lax.rem(tile_id, 2)
    rows, dim = e_ref.shape
    tile = z_ref.shape[-1]
    per_block = dim // tile

    def copies(step, at):
        block, part = lax.div(step, per_block), lax.rem(step, per_block)
        off = pl.multiple_of(part * tile, tile)
        return (
            pltpu.make_async_copy(g1_scr.at[at], g_hbm.at[block, :, pl.ds(off, tile)], sems.at[0, at]),
            pltpu.make_async_copy(g2_scr.at[at], g_hbm.at[blocks + block, pl.ds(off, tile), :], sems.at[1, at]),
        )

    @pl.when(tile_id == 0)
    def _():
        eb_scr[...] = e_ref[...].astype(BF)
        e_out[...] = e_ref[...]

    @pl.when(tile_id >= 2)
    def _():
        for item in copies(tile_id - 2, slot):
            item.wait()

    w1 = w1_ref[0].astype(BF)
    w2 = w2_ref[0].astype(BF)
    for start in range(0, rows, chunk):
        part = slice(start, start + chunk)
        q = dot(eb_scr[part, :], w2, COLS_BOTH)
        z = z_ref[0, part, :]
        t = gelu_tanh(z)
        cdf = 0.5 * (1.0 + t)
        a_scr[part, :] = (z * cdf).astype(BF)
        slope = cdf + (z * (0.5 * (1.0 - t * t))) * (GELU_C * (1.0 + (3.0 * GELU_K) * (z * z)))
        s = (slope * q).astype(BF)
        s_scr[part, :] = s
        e_out[part, :] += dot(s, w1, COLS_BOTH)
    g1_scr[slot] = dot(hb_ref[0], s_scr[...], ROWS_BOTH).astype(BF)
    g2_scr[slot] = dot(a_scr[...], eb_scr[...], ROWS_BOTH).astype(BF)
    for item in copies(tile_id, slot):
        item.start()

    @pl.when(tile_id == pl.num_programs(0) - 1)
    def _():
        for item in copies(tile_id - 1, 1 - slot):
            item.wait()
        for item in copies(tile_id, slot):
            item.wait()


def backward_layer(layer, e, hb, w_in, w_out, z, tile=512, chunk=256):
    dim, hidden = w_in.shape[1:]
    rows = e.shape[0]
    blocks = hidden // dim
    whole = pl.BlockSpec((rows, dim), lambda j, lay: (0, 0))
    return pl.pallas_call(
        functools.partial(backward_body, blocks, chunk),
        grid_spec=pltpu.PrefetchScalarGridSpec(
            num_scalar_prefetch=1,
            grid=(hidden // tile,),
            in_specs=[
                whole,
                pl.BlockSpec((1, rows, dim), lambda j, lay: (lay[0], 0, 0)),
                pl.BlockSpec((1, dim, tile), lambda j, lay: (lay[0], 0, j)),
                pl.BlockSpec((1, tile, dim), lambda j, lay: (lay[0], j, 0)),
                pl.BlockSpec((1, rows, tile), lambda j, lay: (lay[0], 0, j)),
            ],
            out_specs=[pl.BlockSpec(memory_space=pl.ANY), whole],
            scratch_shapes=[
                pltpu.VMEM((rows, dim), BF),
                pltpu.VMEM((rows, tile), BF),
                pltpu.VMEM((rows, tile), BF),
                pltpu.VMEM((2, dim, tile), BF),
                pltpu.VMEM((2, tile, dim), BF),
                pltpu.SemaphoreType.DMA((2, 2)),
            ],
        ),
        out_shape=[
            jax.ShapeDtypeStruct((2 * blocks, dim, dim), BF),
            jax.ShapeDtypeStruct((rows, dim), F32),
        ],
        compiler_params=pltpu.CompilerParams(dimension_semantics=("arbitrary",), vmem_limit_bytes=VMEM_LIMIT),
        cost_estimate=cost(8 * rows * dim * hidden, 12 * dim * hidden + 4 * rows * hidden),
        name="backward_layer",
    )(jnp.full((1,), layer, jnp.int32), e, hb, w_in, w_out, z)


def update_body(step_size, first, chunk, layer_ref, h_ref, w1_ref, m1_ref, g1_ref, w2_ref, m2_ref, g2_ref, *rest):
    w1_out, w2_out, m1_out, m2_out, h_out, hb_scr = rest[0 if first else 4 :]
    tile_id = pl.program_id(0)

    @pl.when(tile_id == 0)
    def _():
        hb_scr[...] = h_ref[...].astype(BF)
        h_out[...] = h_ref[...].astype(F32)

    m1 = MOMENTUM * m1_ref[0] + g1_ref[0].astype(F32)
    m1_out[0] = m1
    w1 = w1_ref[0] - step_size * m1
    w1_out[0] = w1
    m2 = MOMENTUM * m2_ref[0] + g2_ref[0].astype(F32)
    m2_out[0] = m2
    w2 = w2_ref[0] - step_size * m2
    w2_out[0] = w2
    w1 = w1.astype(BF)
    w2 = w2.astype(BF)
    rows = h_ref.shape[0]
    for start in range(0, rows, chunk):
        part = slice(start, start + chunk)
        z = dot(hb_scr[part, :], w1)
        h_out[part, :] += dot(gelu(z).astype(BF), w2)


def update_layer(layer, h, w_in, w_out, mom_in, mom_out, grads, olds, step_size, tile=256, chunk=512):
    _, dim, hidden = w_in.shape
    rows = h.shape[0]
    blocks = hidden // dim
    per_block = dim // tile
    first = olds is None
    whole = pl.BlockSpec((rows, dim), lambda j, lay: (0, 0))
    cols = pl.BlockSpec((1, dim, tile), lambda j, lay: (lay[0], 0, j))
    rws = pl.BlockSpec((1, tile, dim), lambda j, lay: (lay[0], j, 0))
    g_cols = pl.BlockSpec((1, dim, tile), lambda j, lay: (j // per_block, 0, j % per_block))
    g_rows = pl.BlockSpec((1, tile, dim), lambda j, lay: (blocks + j // per_block, j % per_block, 0))
    anyspec = pl.BlockSpec(memory_space=pl.ANY)
    shape_in = jax.ShapeDtypeStruct(w_in.shape, F32)
    shape_out = jax.ShapeDtypeStruct(w_out.shape, F32)
    out = pl.pallas_call(
        functools.partial(update_body, step_size, first, chunk),
        grid_spec=pltpu.PrefetchScalarGridSpec(
            num_scalar_prefetch=1,
            grid=(hidden // tile,),
            in_specs=[whole, cols, cols, g_cols, rws, rws, g_rows] + ([] if first else [anyspec] * 4),
            out_specs=[cols, rws, cols, rws, whole],
            scratch_shapes=[pltpu.VMEM((rows, dim), BF)],
        ),
        out_shape=[shape_in, shape_out, shape_in, shape_out, jax.ShapeDtypeStruct((rows, dim), F32)],
        input_output_aliases={} if first else {8: 0, 9: 1, 10: 2, 11: 3},
        compiler_params=pltpu.CompilerParams(dimension_semantics=("arbitrary",), vmem_limit_bytes=VMEM_LIMIT),
        cost_estimate=cost(4 * rows * dim * hidden, 36 * dim * hidden),
        name="update_layer",
    )(jnp.full((1,), layer, jnp.int32), h, w_in, mom_in, grads, w_out, mom_out, grads, *(() if first else olds))
    return out[:4], out[4]


def solution(mesh):
    groups = mesh.shape["data"]
    rows_spec = P("data", None)

    def local_steps(w_in, w_out, mom_in, mom_out, x_first, y_first, x_second, y_second):
        layers = w_in.shape[0]
        tok_local, model_dim = x_first.shape
        step_size = LR_SCALE / layers
        z, hb, err = forward_first(x_first, y_first, w_in, w_out, 1.0 / (tok_local * groups * model_dim))
        sums = [None] * layers
        for layer in reversed(range(layers)):
            grads, err = backward_layer(layer, err, hb, w_in, w_out, z)
            shard = lax.psum_scatter(grads, "data", scatter_dimension=0, tiled=True)
            sums[layer] = lax.all_gather(shard, "data", axis=0, tiled=True)
        olds, h = None, x_second
        for layer in range(layers):
            olds, h = update_layer(layer, h, w_in, w_out, mom_in, mom_out, sums[layer], olds, step_size)
        row_diff = h - y_second.astype(F32)
        loss_rows = jnp.sum(row_diff * row_diff, axis=-1) / (2 * model_dim)
        w_in_new, w_out_new, mom_in_new, mom_out_new = olds
        return w_in_new, w_out_new, mom_in_new, mom_out_new, loss_rows, h

    return jax.shard_map(local_steps, mesh=mesh, in_specs=(P(), P(), P(), P(), rows_spec, rows_spec, rows_spec, rows_spec), out_specs=(P(), P(), P(), P(), P("data"), rows_spec), check_vma=False)
```

time: 3450 us -> 2300 us (0.67)
  Pallas kernels: 0 us -> 1110 us
  matrix products: 1070 us -> 0 us
  local copies, waits for them, and re-layouts: 634 us -> 0.01 us
  other arithmetic: 552 us -> 3.4 us
    psum x2 -> x0, waiting for transfers between devices: 1170 us -> none  [local_steps(): lax.psum((grad_in, grad_out), 'data')]
    pallas_call x0 -> x17, Pallas kernels: none -> 1110 us  [the longest x8 479 us: update_layer(): pl.pallas_call(functools.partial(update_body, step_size, first, chunk), g...]
    dot_general x60 -> x0, matrix products: 1070 us -> none  [the longest x16 292 us: forward_stack(): h_cur = h_cur + jnp.dot(act_bf, w_out_l, preferred_element_type=jnp.float32)]
    reduce_scatter x0 -> x8, waiting for transfers between devices: none -> 886 us  [local_steps(): shard = lax.psum_scatter(grads, 'data', scatter_dimension=0, tiled=True)]
    unnamed x75 -> x2, local copies, waits for them, and re-layouts: 619 us -> 0.01 us
    another operation x4 -> x0, other arithmetic: 552 us -> none
    all_gather x0 -> x8, waiting for transfers between devices: none -> 266 us  [local_steps(): sums[layer] = lax.all_gather(shard, 'data', axis=0, tiled=True)]
  transfers between devices with their start and end apart: 2 -> 16, of which waited for: 2 -> 16; matrix products, arithmetic and copies ran while one was open for 10% -> 0% of each run, Pallas kernels for 0% -> 18%
where the time goes in v1:
time: 2300 us; the launch traced here: 2290 us
  waiting for transfers between devices  1160 us (50%)
  Pallas kernels  1110 us (48%)
    reduce_scatter x8, waiting for transfers between devices, local_steps(): shard = lax.psum_scatter(grads, 'data', scatter_dimension=0, tiled=True)  886 us
    pallas_call x8, Pallas kernels, update_layer(): pl.pallas_call(functools.partial(update_body, step_size, first, chunk), g...  479 us
    pallas_call x8, Pallas kernels, backward_layer(): pl.pallas_call(functools.partial(backward_body, blocks, chunk), grid_spec...  430 us
    all_gather x8, waiting for transfers between devices, local_steps(): sums[layer] = lax.all_gather(shard, 'data', axis=0, tiled=True)  266 us
    pallas_call x1, Pallas kernels, forward_first(): pl.pallas_call(functools.partial(forward_body, err_scale, chunk), grid=(l...  206 us
  transfers between devices with their start and end apart: 16, of which 16 were waited for; matrix products, arithmetic and copies ran while one was open for 0% of the time, Pallas kernels for 18%

profile of v1, /device:TPU:0, one launch (start us, length us, event | category | flops | bytes accessed | tf_op | source)
XLA Modules:
  0.0 2288.8 jit_solution(7664760007056267704)
XLA Ops:
  7.2 205.9 %forward_first.1 = (f32[8,1024,4096]{2,1,0:T(8,128)}, bf16[8,1024,1024]{2,1,0:T(8,128)(2,1)}, f32[1024,1024]{1,0:T(8,128)}) custom-call(bf16[1024,1024]{1,0:T(8,128)(2,1)} %x_ref.1, bf16[1024,1024]{1,0:T(8,128)(2,1)} %y_ref.1, f32[8,1024,4096]{2,1,0:T(8,128)} %w1_ref.33, f32[8,4096,1024]{2,1,0:T(8,128)} %w2_ref.33), custom_call_target="tpu_custom_call" | custom-call | flops 137438953472 | bytes 402653184 | tf_op jit(solution)/shard_map/forward_first/pallas_call | solution.py:70
  266.7 54.0 %backward_layer.9 = (bf16[8,1024,1024]{2,1,0:T(8,128)(2,1)}, f32[1024,1024]{1,0:T(8,128)}) custom-call(s32[1]{0:T(128)} %constant.2.clone.1.layer_ref, f32[1024,1024]{1,0:T(8,128)} %get-tuple-element.67.e_ref, bf16[8,1024,1024]{2,1,0:T(8,128)(2,1)} %get-tuple-element.65.hb_ref, f32[8,1024,4096]{2,1,0:T(8,128)} %w1_ref.33, f32[8,4096,1024]{2,1,0:T(8,128)} %w2_ref.33, ...), custom_call_target="tpu_custom_call" | custom-call | flops 34359738368 | bytes 67108864 | tf_op jit(solution)/shard_map/backward_layer/pallas_call | solution.py:154
  320.7 53.6 %backward_layer.10 = (bf16[8,1024,1024]{2,1,0:T(8,128)(2,1)}, f32[1024,1024]{1,0:T(8,128)}) custom-call(s32[1]{0:T(128)} %constant.3.clone.1.layer_ref, f32[1024,1024]{1,0:T(8,128)} %get-tuple-element.68.e_ref, bf16[8,1024,1024]{2,1,0:T(8,128)(2,1)} %get-tuple-element.65.hb_ref, f32[8,1024,4096]{2,1,0:T(8,128)} %w1_ref.33, f32[8,4096,1024]{2,1,0:T(8,128)} %w2_ref.33, ...), custom_call_target="tpu_custom_call" | custom-call | flops 34359738368 | bytes 67108864 | tf_op jit(solution)/shard_map/backward_layer/pallas_call | solution.py:154
  374.3 53.8 %backward_layer.11 = (bf16[8,1024,1024]{2,1,0:T(8,128)(2,1)}, f32[1024,1024]{1,0:T(8,128)}) custom-call(s32[1]{0:T(128)} %constant.4.clone.1.layer_ref, f32[1024,1024]{1,0:T(8,128)} %get-tuple-element.69.e_ref, bf16[8,1024,1024]{2,1,0:T(8,128)(2,1)} %get-tuple-element.65.hb_ref, f32[8,1024,4096]{2,1,0:T(8,128)} %w1_ref.33, f32[8,4096,1024]{2,1,0:T(8,128)} %w2_ref.33, ...), custom_call_target="tpu_custom_call" | custom-call | flops 34359738368 | bytes 67108864 | tf_op jit(solution)/shard_map/backward_layer/pallas_call | solution.py:154
  481.6 53.8 %backward_layer.13 = (bf16[8,1024,1024]{2,1,0:T(8,128)(2,1)}, f32[1024,1024]{1,0:T(8,128)}) custom-call(s32[1]{0:T(128)} %constant.6.clone.1.layer_ref, f32[1024,1024]{1,0:T(8,128)} %get-tuple-element.71.e_ref, bf16[8,1024,1024]{2,1,0:T(8,128)(2,1)} %get-tuple-element.65.hb_ref, f32[8,1024,4096]{2,1,0:T(8,128)} %w1_ref.33, f32[8,4096,1024]{2,1,0:T(8,128)} %w2_ref.33, ...), custom_call_target="tpu_custom_call" | custom-call | flops 34359738368 | bytes 67108864 | tf_op jit(solution)/shard_map/backward_layer/pallas_call | solution.py:154
  535.3 53.6 %backward_layer.14 = (bf16[8,1024,1024]{2,1,0:T(8,128)(2,1)}, f32[1024,1024]{1,0:T(8,128)}) custom-call(s32[1]{0:T(128)} %constant.7.clone.1.layer_ref, f32[1024,1024]{1,0:T(8,128)} %get-tuple-element.72.e_ref, bf16[8,1024,1024]{2,1,0:T(8,128)(2,1)} %get-tuple-element.65.hb_ref, f32[8,1024,4096]{2,1,0:T(8,128)} %w1_ref.33, f32[8,4096,1024]{2,1,0:T(8,128)} %w2_ref.33, ...), custom_call_target="tpu_custom_call" | custom-call | flops 34359738368 | bytes 67108864 | tf_op jit(solution)/shard_map/backward_layer/pallas_call | solution.py:154
  588.9 54.0 %backward_layer.15 = (bf16[8,1024,1024]{2,1,0:T(8,128)(2,1)}, f32[1024,1024]{1,0:T(8,128)}) custom-call(s32[1]{0:T(128)} %constant.8.clone.1.layer_ref, f32[1024,1024]{1,0:T(8,128)} %get-tuple-element.73.e_ref, bf16[8,1024,1024]{2,1,0:T(8,128)(2,1)} %get-tuple-element.65.hb_ref, f32[8,1024,4096]{2,1,0:T(8,128)} %w1_ref.33, f32[8,4096,1024]{2,1,0:T(8,128)} %w2_ref.33, ...), custom_call_target="tpu_custom_call" | custom-call | flops 34359738368 | bytes 67108864 | tf_op jit(solution)/shard_map/backward_layer/pallas_call | solution.py:154
  647.7 106.0 %reduce-scatter.9.cloned.1.call-done = bf16[1,1024,1024]{2,1,0:T(8,128)(2,1)} async-done(((bf16[8,1024,1024]{2,1,0:T(8,128)(2,1)}), bf16[1,1024,1024]{2,1,0:T(8,128)(2,1)}) %reduce-scatter.9.cloned.1.call-update) | async-done | bytes 2097168 | tf_op jit(solution)/shard_map/reduce_scatter | solution.py:256
  753.8 111.3 %reduce-scatter.11.cloned.1.call-done = bf16[1,1024,1024]{2,1,0:T(8,128)(2,1)} async-done(((bf16[8,1024,1024]{2,1,0:T(8,128)(2,1)}), bf16[1,1024,1024]{2,1,0:T(8,128)(2,1)}) %reduce-scatter.11.cloned.1.call-update) | async-done | bytes 2097168 | tf_op jit(solution)/shard_map/reduce_scatter | solution.py:256
  865.2 111.3 %reduce-scatter.13.cloned.1.call-done = bf16[1,1024,1024]{2,1,0:T(8,128)(2,1)} async-done(((bf16[8,1024,1024]{2,1,0:T(8,128)(2,1)}), bf16[1,1024,1024]{2,1,0:T(8,128)(2,1)}) %reduce-scatter.13.cloned.1.call-update) | async-done | bytes 2097168 | tf_op jit(solution)/shard_map/reduce_scatter | solution.py:256
  976.6 111.2 %reduce-scatter.15.cloned.1.call-done = bf16[1,1024,1024]{2,1,0:T(8,128)(2,1)} async-done(((bf16[8,1024,1024]{2,1,0:T(8,128)(2,1)}), bf16[1,1024,1024]{2,1,0:T(8,128)(2,1)}) %reduce-scatter.15.cloned.1.call-update) | async-done | bytes 2097168 | tf_op jit(solution)/shard_map/reduce_scatter | solution.py:256
  1087.9 111.2 %reduce-scatter.17.cloned.1.call-done = bf16[1,1024,1024]{2,1,0:T(8,128)(2,1)} async-done(((bf16[8,1024,1024]{2,1,0:T(8,128)(2,1)}), bf16[1,1024,1024]{2,1,0:T(8,128)(2,1)}) %reduce-scatter.17.cloned.1.call-update) | async-done | bytes 2097168 | tf_op jit(solution)/shard_map/reduce_scatter | solution.py:256
  1199.1 111.2 %reduce-scatter.19.cloned.1.call-done = bf16[1,1024,1024]{2,1,0:T(8,128)(2,1)} async-done(((bf16[8,1024,1024]{2,1,0:T(8,128)(2,1)}), bf16[1,1024,1024]{2,1,0:T(8,128)(2,1)}) %reduce-scatter.19.cloned.1.call-update) | async-done | bytes 2097168 | tf_op jit(solution)/shard_map/reduce_scatter | solution.py:256
  1310.3 111.9 %reduce-scatter.21.cloned.1.call-done = bf16[1,1024,1024]{2,1,0:T(8,128)(2,1)} async-done(((bf16[8,1024,1024]{2,1,0:T(8,128)(2,1)}), bf16[1,1024,1024]{2,1,0:T(8,128)(2,1)}) %reduce-scatter.21.cloned.1.call-update) | async-done | bytes 2097168 | tf_op jit(solution)/shard_map/reduce_scatter | solution.py:256
  1422.3 111.9 %reduce-scatter.23.cloned.1.call-done = bf16[1,1024,1024]{2,1,0:T(8,128)(2,1)} async-done(((bf16[8,1024,1024]{2,1,0:T(8,128)(2,1)}), bf16[1,1024,1024]{2,1,0:T(8,128)(2,1)}) %reduce-scatter.23.cloned.1.call-update) | async-done | bytes 2097168 | tf_op jit(solution)/shard_map/reduce_scatter | solution.py:256
  1534.2 86.0 %all-gather.9.cloned.1.call-done.g1_ref.g2_ref = bf16[8,1024,1024]{2,1,0:T(8,128)(2,1)} async-done(((bf16[1,1024,1024]{2,1,0:T(8,128)(2,1)}), bf16[8,1024,1024]{2,1,0:T(8,128)(2,1)}) %all-gather.9.cloned.1.call-update) | async-done | bytes 16777232 | tf_op jit(solution)/shard_map/all_gather | solution.py:257
  1620.2 59.9 %update_layer.8 = (f32[8,1024,4096]{2,1,0:T(8,128)}, f32[8,4096,1024]{2,1,0:T(8,128)}, f32[8,1024,4096]{2,1,0:T(8,128)}, f32[8,4096,1024]{2,1,0:T(8,128)}, f32[1024,1024]{1,0:T(8,128)}) custom-call(s32[1]{0:T(128)} %constant.8.clone.1.layer_ref, bf16[1024,1024]{1,0:T(8,128)(2,1)} %h_ref.1, f32[8,1024,4096]{2,1,0:T(8,128)} %w1_ref.33, ...), custom_call_target="tpu_custom_call" | custom-call | flops 17179869184 | bytes 150994944 | tf_op jit(solution)/shard_map/update_layer/pallas_call | solution.py:226
  1706.1 60.2 %update_layer.9 = (f32[8,1024,4096]{2,1,0:T(8,128)}, f32[8,4096,1024]{2,1,0:T(8,128)}, f32[8,1024,4096]{2,1,0:T(8,128)}, f32[8,4096,1024]{2,1,0:T(8,128)}, f32[1024,1024]{1,0:T(8,128)}) custom-call(s32[1]{0:T(128)} %constant.7.clone.1.layer_ref, ...), custom_call_target="tpu_custom_call", output_to_operand_aliasing={{0}: (8, {}), {1}: (9, {}), {2}: (10, {}), {3}: (11, {})} | custom-call | flops 17179869184 | bytes 150994944 | tf_op jit(solution)/shard_map/update_layer/pallas_call | solution.py:226
  1792.1 60.3 %update_layer.10 = (f32[8,1024,4096]{2,1,0:T(8,128)}, f32[8,4096,1024]{2,1,0:T(8,128)}, f32[8,1024,4096]{2,1,0:T(8,128)}, f32[8,4096,1024]{2,1,0:T(8,128)}, f32[1024,1024]{1,0:T(8,128)}) custom-call(s32[1]{0:T(128)} %constant.6.clone.1.layer_ref, ...), custom_call_target="tpu_custom_call", output_to_operand_aliasing={{0}: (8, {}), {1}: (9, {}), {2}: (10, {}), {3}: (11, {})} | custom-call | flops 17179869184 | bytes 150994944 | tf_op jit(solution)/shard_map/update_layer/pallas_call | solution.py:226
  1878.0 60.3 %update_layer.11 = (f32[8,1024,4096]{2,1,0:T(8,128)}, f32[8,4096,1024]{2,1,0:T(8,128)}, f32[8,1024,4096]{2,1,0:T(8,128)}, f32[8,4096,1024]{2,1,0:T(8,128)}, f32[1024,1024]{1,0:T(8,128)}) custom-call(s32[1]{0:T(128)} %constant.5.clone.1.layer_ref, ...), custom_call_target="tpu_custom_call", output_to_operand_aliasing={{0}: (8, {}), {1}: (9, {}), {2}: (10, {}), {3}: (11, {})} | custom-call | flops 17179869184 | bytes 150994944 | tf_op jit(solution)/shard_map/update_layer/pallas_call | solution.py:226
  1964.0 60.5 %update_layer.12 = (f32[8,1024,4096]{2,1,0:T(8,128)}, f32[8,4096,1024]{2,1,0:T(8,128)}, f32[8,1024,4096]{2,1,0:T(8,128)}, f32[8,4096,1024]{2,1,0:T(8,128)}, f32[1024,1024]{1,0:T(8,128)}) custom-call(s32[1]{0:T(128)} %constant.4.clone.1.layer_ref, ...), custom_call_target="tpu_custom_call", output_to_operand_aliasing={{0}: (8, {}), {1}: (9, {}), {2}: (10, {}), {3}: (11, {})} | custom-call | flops 17179869184 | bytes 150994944 | tf_op jit(solution)/shard_map/update_layer/pallas_call | solution.py:226
  2049.9 60.3 %update_layer.13 = (f32[8,1024,4096]{2,1,0:T(8,128)}, f32[8,4096,1024]{2,1,0:T(8,128)}, f32[8,1024,4096]{2,1,0:T(8,128)}, f32[8,4096,1024]{2,1,0:T(8,128)}, f32[1024,1024]{1,0:T(8,128)}) custom-call(s32[1]{0:T(128)} %constant.3.clone.1.layer_ref, ...), custom_call_target="tpu_custom_call", output_to_operand_aliasing={{0}: (8, {}), {1}: (9, {}), {2}: (10, {}), {3}: (11, {})} | custom-call | flops 17179869184 | bytes 150994944 | tf_op jit(solution)/shard_map/update_layer/pallas_call | solution.py:226
  2135.8 60.3 %update_layer.14 = (f32[8,1024,4096]{2,1,0:T(8,128)}, f32[8,4096,1024]{2,1,0:T(8,128)}, f32[8,1024,4096]{2,1,0:T(8,128)}, f32[8,4096,1024]{2,1,0:T(8,128)}, f32[1024,1024]{1,0:T(8,128)}) custom-call(s32[1]{0:T(128)} %constant.2.clone.1.layer_ref, ...), custom_call_target="tpu_custom_call", output_to_operand_aliasing={{0}: (8, {}), {1}: (9, {}), {2}: (10, {}), {3}: (11, {})} | custom-call | flops 17179869184 | bytes 150994944 | tf_op jit(solution)/shard_map/update_layer/pallas_call | solution.py:226
  2221.6 57.0 %update_layer.15 = (f32[8,1024,4096]{2,1,0:T(8,128)}, f32[8,4096,1024]{2,1,0:T(8,128)}, f32[8,1024,4096]{2,1,0:T(8,128)}, f32[8,4096,1024]{2,1,0:T(8,128)}, f32[1024,1024]{1,0:T(8,128)}) custom-call(s32[1]{0:T(128)} %constant.1.clone.1.layer_ref, ...), custom_call_target="tpu_custom_call", output_to_operand_aliasing={{0}: (8, {}), {1}: (9, {}), {2}: (10, {}), {3}: (11, {})} | custom-call | flops 17179869184 | bytes 150994944 | tf_op jit(solution)/shard_map/update_layer/pallas_call | solution.py:226
  (45 shorter events, 295.1 us)
Async XLA Ops:
  7.2 746.6 %reduce-scatter.9.cloned.1.call-start = ((), (), s32[]{:S(2)}) async-start(), calls=%async_computation.8 | async-start | bytes 18874368 | tf_op jit(solution)/shard_map/reduce_scatter | solution.py:256
  643.0 222.2 %reduce-scatter.11.cloned.1.call-start = ((), (), s32[]{:S(2)}) async-start(), calls=%async_computation.10 | async-start | bytes 18874368 | tf_op jit(solution)/shard_map/reduce_scatter | solution.py:256
  643.7 332.8 %reduce-scatter.13.cloned.1.call-start = ((), (), s32[]{:S(2)}) async-start(), calls=%async_computation.12 | async-start | bytes 18874368 | tf_op jit(solution)/shard_map/reduce_scatter | solution.py:256
  644.5 443.3 %reduce-scatter.15.cloned.1.call-start = ((), (), s32[]{:S(2)}) async-start(), calls=%async_computation.14 | async-start | bytes 18874368 | tf_op jit(solution)/shard_map/reduce_scatter | solution.py:256
  645.0 554.0 %reduce-scatter.17.cloned.1.call-start = ((), (), s32[]{:S(2)}) async-start(), calls=%async_computation.16 | async-start | bytes 18874368 | tf_op jit(solution)/shard_map/reduce_scatter | solution.py:256
  645.6 664.7 %reduce-scatter.19.cloned.1.call-start = ((), (), s32[]{:S(2)}) async-start(), calls=%async_computation.18 | async-start | bytes 18874368 | tf_op jit(solution)/shard_map/reduce_scatter | solution.py:256
  646.2 776.0 %reduce-scatter.21.cloned.1.call-start = ((), (), s32[]{:S(2)}) async-start(), calls=%async_computation.20 | async-start | bytes 18874368 | tf_op jit(solution)/shard_map/reduce_scatter | solution.py:256
  646.9 887.3 %reduce-scatter.23.cloned.1.call-start = ((), (), s32[]{:S(2)}) async-start(), calls=%async_computation.22 | async-start | bytes 18874368 | tf_op jit(solution)/shard_map/reduce_scatter | solution.py:256
  647.7 972.5 %all-gather.9.cloned.1.call-start = ((), (), s32[]{:S(2)}) async-start(), calls=%async_computation.9 | async-start | bytes 18874368 | tf_op jit(solution)/shard_map/all_gather | solution.py:257
  753.8 952.3 %all-gather.11.cloned.1.call-start = ((), (), s32[]{:S(2)}) async-start(), calls=%async_computation.11 | async-start | bytes 18874368 | tf_op jit(solution)/shard_map/all_gather | solution.py:257
  865.2 926.9 %all-gather.13.cloned.1.call-start = ((), (), s32[]{:S(2)}) async-start(), calls=%async_computation.13 | async-start | bytes 18874368 | tf_op jit(solution)/shard_map/all_gather | solution.py:257
  976.6 901.4 %all-gather.15.cloned.1.call-start = ((), (), s32[]{:S(2)}) async-start(), calls=%async_computation.15 | async-start | bytes 18874368 | tf_op jit(solution)/shard_map/all_gather | solution.py:257
  1087.8 876.2 %all-gather.17.cloned.1.call-start = ((), (), s32[]{:S(2)}) async-start(), calls=%async_computation.17 | async-start | bytes 18874368 | tf_op jit(solution)/shard_map/all_gather | solution.py:257
  1199.1 850.8 %all-gather.19.cloned.1.call-start = ((), (), s32[]{:S(2)}) async-start(), calls=%async_computation.19 | async-start | bytes 18874368 | tf_op jit(solution)/shard_map/all_gather | solution.py:257
  1310.3 825.5 %all-gather.21.cloned.1.call-start = ((), (), s32[]{:S(2)}) async-start(), calls=%async_computation.21 | async-start | bytes 18874368 | tf_op jit(solution)/shard_map/all_gather | solution.py:257
  1422.3 799.4 %all-gather.23.cloned.1.call-start = ((), (), s32[]{:S(2)}) async-start(), calls=%async_computation.23 | async-start | bytes 18874368 | tf_op jit(solution)/shard_map/all_gather | solution.py:257
  2221.6 57.0 %copy-start = (bf16[1024,1024]{1,0:T(8,128)(2,1)S(1)}, bf16[1024,1024]{1,0:T(8,128)(2,1)}, u32[]{:S(2)}) copy-start(bf16[1024,1024]{1,0:T(8,128)(2,1)} %param.15) | copy-start | bytes 6291460
Sparse Core Ops, SparseCore 0:
  643.1 110.6 reduce-scatter.8
  757.3 107.8 reduce-scatter.10
  868.7 107.8 reduce-scatter.12
  979.9 107.8 reduce-scatter.14
  1091.1 107.8 reduce-scatter.16
  1202.4 107.8 reduce-scatter.18
  1314.3 107.8 reduce-scatter.20
  1426.3 107.8 reduce-scatter.22
  1536.0 84.1 all-gather.8
  1621.9 84.1 all-gather.10
  1707.9 84.1 all-gather.12
  1793.8 84.1 all-gather.14
  1879.8 84.1 all-gather.16
  1965.7 84.1 all-gather.18
  2051.6 84.1 all-gather.20
  2137.4 84.1 all-gather.22

commit v2 on v1

v2 whole, which is shorter than its diff:
```python
import functools
import math

import jax
import jax.numpy as jnp
from jax import lax
from jax.experimental import pallas as pl
from jax.experimental.pallas import tpu as pltpu
from jax.sharding import Mesh, PartitionSpec as P


LR_SCALE = 1.0
MOMENTUM = 0.9
GELU_C = math.sqrt(2.0 / math.pi)
GELU_K = 0.044715
BF = jnp.bfloat16
F32 = jnp.float32
ROWS_BOTH = (((0,), (0,)), ((), ()))
COLS_BOTH = (((1,), (1,)), ((), ()))
PLAIN = (((1,), (0,)), ((), ()))
VMEM_LIMIT = 60 * 1024 * 1024


def dot(a, b, dims=PLAIN):
    return lax.dot_general(a, b, dims, preferred_element_type=F32)


def gelu_tanh(z):
    return jnp.tanh(GELU_C * (z + GELU_K * (z * z * z)))


def gelu(z):
    return z * (0.5 * (1.0 + gelu_tanh(z)))


def cost(flops, nbytes):
    return pl.CostEstimate(flops=int(flops), bytes_accessed=int(nbytes), transcendentals=0)


def forward_body(err_scale, chunk, x_ref, y_ref, w1_ref, w2_ref, z_ref, hb_ref, e_ref, h_scr, hb_scr):
    layer, tile = pl.program_id(0), pl.program_id(1)

    @pl.when((layer == 0) & (tile == 0))
    def _():
        h_scr[...] = x_ref[...].astype(F32)

    @pl.when(tile == 0)
    def _():
        hb = h_scr[...].astype(BF)
        hb_scr[...] = hb
        hb_ref[0] = hb

    w1 = w1_ref[0].astype(BF)
    w2 = w2_ref[0].astype(BF)
    rows = h_scr.shape[0]
    for start in range(0, rows, chunk):
        z = dot(hb_scr[start : start + chunk, :], w1)
        z_ref[0, start : start + chunk, :] = z
        h_scr[start : start + chunk, :] += dot(gelu(z).astype(BF), w2)

    @pl.when((layer == pl.num_programs(0) - 1) & (tile == pl.num_programs(1) - 1))
    def _():
        e_ref[...] = (h_scr[...] - y_ref[...].astype(F32)) * err_scale


def forward_first(x, y, w_in, w_out, err_scale, tile=512, chunk=1024):
    layers, dim, hidden = w_in.shape
    rows = x.shape[0]
    whole = pl.BlockSpec((rows, dim), lambda l, j: (0, 0))
    return pl.pallas_call(
        functools.partial(forward_body, err_scale, chunk),
        grid=(layers, hidden // tile),
        in_specs=[
            whole,
            whole,
            pl.BlockSpec((1, dim, tile), lambda l, j: (l, 0, j)),
            pl.BlockSpec((1, tile, dim), lambda l, j: (l, j, 0)),
        ],
        out_specs=[
            pl.BlockSpec((1, rows, tile), lambda l, j: (l, 0, j)),
            pl.BlockSpec((1, rows, dim), lambda l, j: (l, 0, 0)),
            whole,
        ],
        out_shape=[
            jax.ShapeDtypeStruct((layers, rows, hidden), F32),
            jax.ShapeDtypeStruct((layers, rows, dim), BF),
            jax.ShapeDtypeStruct((rows, dim), F32),
        ],
        scratch_shapes=[pltpu.VMEM((rows, dim), F32), pltpu.VMEM((rows, dim), BF)],
        compiler_params=pltpu.CompilerParams(
            dimension_semantics=("arbitrary", "arbitrary"), vmem_limit_bytes=VMEM_LIMIT
        ),
        cost_estimate=cost(4 * layers * rows * dim * hidden, layers * (8 * dim * hidden + 4 * rows * hidden)),
        name="forward_first",
    )(x, y, w_in, w_out)


def device_bits():
    return tuple(lax.axis_index(name) for name in ("core", "x", "y"))


def tile_of(step):
    core, x, y = device_bits()
    side = lax.rem(core + lax.div(step, 4) + 1, 2)
    near, far = x * (1 - side) + y * side, y * (1 - side) + x * side
    rest = lax.rem(step, 4)
    near = lax.rem(near + lax.div(rest, 2) + 1, 2)
    far = lax.rem(far + lax.rem(rest, 2) + 1, 2)
    return 4 * side + 2 * (far * (1 - side) + near * side) + near * (1 - side) + far * side


def backward_body(e_ref, hb_ref, w1_ref, w2_ref, z_ref, near_hbm, far_hbm, own_hbm, e_out, eb_scr, a_scr, s_scr, g_scr, got_scr, out_sems, send_sems, recv_sems):
    step = pl.program_id(0)
    slot = lax.rem(step, 2)
    tile = z_ref.shape[-1]
    partner = {"core": 1 - lax.axis_index("core")}

    def to_partner(at, unit):
        return pltpu.make_async_remote_copy(
            src_ref=g_scr.at[at],
            dst_ref=got_scr.at[unit],
            send_sem=send_sems.at[at],
            recv_sem=recv_sems.at[unit],
            device_id=partner,
            device_id_type=pl.DeviceIdType.MESH,
        )

    def to_hbm(at, hbm, unit):
        return pltpu.make_async_copy(g_scr.at[at], hbm.at[unit], out_sems.at[at])

    @pl.when(step == 0)
    def _():
        barrier = pltpu.get_barrier_semaphore()
        pl.semaphore_signal(barrier, inc=1, device_id=partner, device_id_type=pl.DeviceIdType.MESH)
        pl.semaphore_wait(barrier, 1)
        eb_scr[...] = e_ref[...].astype(BF)
        e_out[...] = e_ref[...]

    @pl.when((step >= 2) & (step < 6))
    def _():
        to_partner(slot, step - 2).wait_send()

    @pl.when(step >= 6)
    def _():
        to_hbm(slot, own_hbm, 0).wait()

    w1 = w1_ref[0].astype(BF)
    w2 = w2_ref[0].astype(BF)
    q = dot(eb_scr[...], w2, COLS_BOTH)
    z = z_ref[0]
    t = gelu_tanh(z)
    cdf = 0.5 * (1.0 + t)
    a_scr[...] = (z * cdf).astype(BF)
    slope = cdf + (z * (0.5 * (1.0 - t * t))) * (GELU_C * (1.0 + (3.0 * GELU_K) * (z * z)))
    s_scr[...] = (slope * q).astype(BF)
    e_out[...] += dot(s_scr[...], w1, COLS_BOTH)
    g_scr[slot, 0] = dot(hb_ref[0], s_scr[...], ROWS_BOTH).astype(BF)
    g2 = dot(a_scr[...], eb_scr[...], ROWS_BOTH).astype(BF)
    g_scr[slot, 1, :tile, :] = g2[:, :tile]
    g_scr[slot, 1, tile:, :] = g2[:, tile:]

    @pl.when(step < 4)
    def _():
        to_partner(slot, step).start()

    @pl.when(step >= 4)
    def _():
        to_partner(slot, step - 4).wait_recv()
        g_scr[slot] = (g_scr[slot].astype(F32) + got_scr[step - 4].astype(F32)).astype(BF)

    @pl.when((step == 4) | (step == 5))
    def _():
        to_hbm(slot, near_hbm, step - 4).start()

    @pl.when(step == 6)
    def _():
        to_hbm(slot, far_hbm, 0).start()

    @pl.when(step == 7)
    def _():
        to_hbm(slot, own_hbm, 0).start()
        to_hbm(1 - slot, far_hbm, 0).wait()
        to_hbm(slot, own_hbm, 0).wait()


def backward_layer(layer, e, hb, w_in, w_out, z):
    dim, hidden = w_in.shape[1:]
    rows = e.shape[0]
    tile = hidden // 8
    whole = pl.BlockSpec((rows, dim), lambda j: (0, 0))
    anyspec = pl.BlockSpec(memory_space=pl.ANY)
    unit = (2, dim, tile)
    return pl.pallas_call(
        backward_body,
        grid=(8,),
        in_specs=[
            whole,
            pl.BlockSpec((1, rows, dim), lambda j: (layer, 0, 0)),
            pl.BlockSpec((1, dim, tile), lambda j: (layer, 0, tile_of(j))),
            pl.BlockSpec((1, tile, dim), lambda j: (layer, tile_of(j), 0)),
            pl.BlockSpec((1, rows, tile), lambda j: (layer, 0, tile_of(j))),
        ],
        out_specs=[anyspec, anyspec, anyspec, whole],
        out_shape=[
            jax.ShapeDtypeStruct((2, *unit), BF),
            jax.ShapeDtypeStruct((1, *unit), BF),
            jax.ShapeDtypeStruct((1, *unit), BF),
            jax.ShapeDtypeStruct((rows, dim), F32),
        ],
        scratch_shapes=[
            pltpu.VMEM((rows, dim), BF),
            pltpu.VMEM((rows, tile), BF),
            pltpu.VMEM((rows, tile), BF),
            pltpu.VMEM((2, *unit), BF),
            pltpu.VMEM((4, *unit), BF),
            pltpu.SemaphoreType.DMA((2,)),
            pltpu.SemaphoreType.DMA((2,)),
            pltpu.SemaphoreType.DMA((4,)),
        ],
        compiler_params=pltpu.CompilerParams(
            dimension_semantics=("arbitrary",), vmem_limit_bytes=VMEM_LIMIT, collective_id=layer, has_side_effects=True
        ),
        cost_estimate=cost(8 * rows * dim * hidden, 12 * dim * hidden + 4 * rows * hidden),
        name="backward_layer",
    )(e, hb, w_in, w_out, z)


def update_body(step_size, first, h_ref, w1_ref, m1_ref, w2_ref, m2_ref, g_ref, *rest):
    w1_out, w2_out, m1_out, m2_out, h_out, hb_scr = rest[0 if first else 4 :]
    tile = g_ref.shape[-1]

    @pl.when(pl.program_id(0) == 0)
    def _():
        hb_scr[...] = h_ref[...].astype(BF)
        h_out[...] = h_ref[...].astype(F32)

    m1 = MOMENTUM * m1_ref[0] + g_ref[0, 0].astype(F32)
    m1_out[0] = m1
    w1 = w1_ref[0] - step_size * m1
    w1_out[0] = w1
    for part in range(2):
        cols = slice(part * tile, (part + 1) * tile)
        m2 = MOMENTUM * m2_ref[0, :, cols] + g_ref[0, 1, cols, :].astype(F32)
        m2_out[0, :, cols] = m2
        w2_out[0, :, cols] = w2_ref[0, :, cols] - step_size * m2
    z = dot(hb_scr[...], w1.astype(BF))
    h_out[...] += dot(gelu(z).astype(BF), w2_out[0].astype(BF))


def update_layer(layer, h, w_in, w_out, mom_in, mom_out, grad, olds, step_size):
    _, dim, hidden = w_in.shape
    rows = h.shape[0]
    tile = hidden // 8
    first = olds is None

    def number(j):
        return 4 * lax.rem(j, 2) + 2 * lax.div(j, 4) + lax.rem(lax.div(j, 2), 2)

    single = pl.BlockSpec((rows, dim), lambda j: (0, 0), pipeline_mode=pl.Buffered(1))
    whole = pl.BlockSpec((rows, dim), lambda j: (0, 0))
    cols = pl.BlockSpec((1, dim, tile), lambda j: (layer, 0, number(j)))
    rws = pl.BlockSpec((1, tile, dim), lambda j: (layer, number(j), 0))
    anyspec = pl.BlockSpec(memory_space=pl.ANY)
    shape_in = jax.ShapeDtypeStruct(w_in.shape, F32)
    shape_out = jax.ShapeDtypeStruct(w_out.shape, F32)
    out = pl.pallas_call(
        functools.partial(update_body, step_size, first),
        grid=(8,),
        in_specs=[single, cols, cols, rws, rws, pl.BlockSpec((1, 2, dim, tile), lambda j: (j, 0, 0, 0))]
        + ([] if first else [anyspec] * 4),
        out_specs=[cols, rws, cols, rws, whole],
        scratch_shapes=[pltpu.VMEM((rows, dim), BF)],
        out_shape=[shape_in, shape_out, shape_in, shape_out, jax.ShapeDtypeStruct((rows, dim), F32)],
        input_output_aliases={} if first else {6 + i: i for i in range(4)},
        compiler_params=pltpu.CompilerParams(dimension_semantics=("arbitrary",), vmem_limit_bytes=VMEM_LIMIT),
        cost_estimate=cost(4 * rows * dim * hidden, 36 * dim * hidden),
        name="update_layer",
    )(h, w_in, mom_in, w_out, mom_out, grad, *(() if first else olds))
    return out[:4], out[4]


AXES = ("y", "x", "core")
SWAP_NEAR = [(i, i ^ (4 if i % 2 else 2)) for i in range(8)]
SWAP_FAR = [(i, i ^ (2 if i % 2 else 4)) for i in range(8)]


def swap(x, perm):
    return lax.ppermute(x, AXES, perm)


def after(value, *others):
    return lax.optimization_barrier((value, *others))[0]


def solution(mesh):
    groups = mesh.shape["data"]
    mesh = Mesh(mesh.devices.reshape(2, 2, 2), AXES)
    rows_spec = P(AXES, None)

    def local_steps(w_in, w_out, mom_in, mom_out, x_first, y_first, x_second, y_second):
        layers = w_in.shape[0]
        tok_local, model_dim = x_first.shape
        step_size = LR_SCALE / layers
        z, hb, err = forward_first(x_first, y_first, w_in, w_out, 1.0 / (tok_local * groups * model_dim))
        near, far, own, shards = {}, {}, {}, {}

        def first_exchange_sum(layer):
            far[layer] = far[layer] + near[layer][:1]
            own[layer] = (own[layer], near[layer][1:], swap(far[layer], SWAP_FAR))

        def second_exchange_sum(layer):
            kept, got_near, got_far = own[layer]
            shards[layer] = kept + got_near + got_far

        for layer in reversed(range(layers)):
            near[layer], far[layer], own[layer], err = backward_layer(layer, err, hb, w_in, w_out, z)
            near[layer] = swap(near[layer], SWAP_NEAR)
            if layer + 1 < layers:
                first_exchange_sum(layer + 1)
                err = after(err, far[layer + 1])
            if layer + 2 < layers:
                second_exchange_sum(layer + 2)
                err = after(err, shards[layer + 2])
        far[0] = after(far[0], far[1])
        second_exchange_sum(1)
        first_exchange_sum(0)
        second_exchange_sum(0)
        olds, h = None, x_second
        for layer in range(layers):
            grad = lax.all_gather(shards[layer], AXES, axis=0, tiled=True)
            olds, h = update_layer(layer, h, w_in, w_out, mom_in, mom_out, grad, olds, step_size)
        row_diff = h - y_second.astype(F32)
        loss_rows = jnp.sum(row_diff * row_diff, axis=-1) / (2 * model_dim)
        w_in_new, w_out_new, mom_in_new, mom_out_new = olds
        return w_in_new, w_out_new, mom_in_new, mom_out_new, loss_rows, h

    return jax.shard_map(local_steps, mesh=mesh, in_specs=(P(), P(), P(), P(), rows_spec, rows_spec, rows_spec, rows_spec), out_specs=(P(), P(), P(), P(), P(AXES), rows_spec), check_vma=False)
```

time: 2300 us -> 1580 us (0.69)
  waiting for transfers between devices: 1160 us -> 402 us
  other arithmetic: 3.4 us -> 55.8 us
  Pallas kernels: 1110 us -> 1080 us
    reduce_scatter x8 -> x0, waiting for transfers between devices: 886 us -> none  [local_steps(): shard = lax.psum_scatter(grads, 'data', scatter_dimension=0, tiled=True)]
    ppermute x0 -> x16, waiting for transfers between devices: none -> 193 us  [swap(): return lax.ppermute(x, AXES, perm)]
    all_gather x8, waiting for transfers between devices: 266 us -> 206 us  [local_steps(): grad = lax.all_gather(shards[layer], AXES, axis=0, tiled=True)]
    add x0 -> x16, other arithmetic: none -> 52.4 us  [the longest x8 29.7 us: second_exchange_sum(): shards[layer] = kept + got_near + got_far]
    pallas_call x16, Pallas kernels: 909 us -> 884 us  [the longest x8 443 us: backward_layer(): pl.pallas_call(backward_body, grid=(8,), in_specs=[whole, pl.BlockSpec((1...]
  transfers between devices with their start and end apart: 16 -> 24, of which waited for: 16 -> 14; matrix products, arithmetic and copies ran while one was open for 0% -> 3% of each run, Pallas kernels for 18% -> 49%
where the time goes in v2:
time: 1580 us; the launch traced here: 1570 us
  Pallas kernels  1080 us (68%)
  waiting for transfers between devices  402 us (25%)
  other arithmetic  55.8 us (4%)
  starting transfers between devices  21.1 us (1%)
    pallas_call x8, Pallas kernels, backward_layer(): pl.pallas_call(backward_body, grid=(8,), in_specs=[whole, pl.BlockSpec((1...  443 us
    pallas_call x8, Pallas kernels, update_layer(): pl.pallas_call(functools.partial(update_body, step_size, first), grid=(8,...  441 us
    all_gather x8, waiting for transfers between devices, local_steps(): grad = lax.all_gather(shards[layer], AXES, axis=0, tiled=True)  206 us
    ppermute x16, waiting for transfers between devices, swap(): return lax.ppermute(x, AXES, perm)  193 us
    pallas_call x1, Pallas kernels, forward_first(): pl.pallas_call(functools.partial(forward_body, err_scale, chunk), grid=(l...  192 us
  transfers between devices with their start and end apart: 24, of which 14 were waited for; matrix products, arithmetic and copies ran while one was open for 3% of the time, Pallas kernels for 49%

profile of v2, /device:TPU:0, one launch (start us, length us, event | category | flops | bytes accessed | tf_op | source)
XLA Modules:
  0.0 1570.4 jit_solution(11734100022734180570)
XLA Ops:
  7.2 191.6 %forward_first.1 = (f32[8,1024,4096]{2,1,0:T(8,128)}, bf16[8,1024,1024]{2,1,0:T(8,128)(2,1)}, f32[1024,1024]{1,0:T(8,128)}) custom-call(bf16[1024,1024]{1,0:T(8,128)(2,1)} %x_ref.1, bf16[1024,1024]{1,0:T(8,128)(2,1)} %y_ref.1, f32[8,1024,4096]{2,1,0:T(8,128)} %w1_ref.33, f32[8,4096,1024]{2,1,0:T(8,128)} %w2_ref.33), custom_call_target="tpu_custom_call" | custom-call | flops 137438953472 | bytes 402653184 | tf_op jit(solution)/shard_map/forward_first/pallas_call | solution.py:70
  198.8 55.7 %backward_layer.8 = (bf16[2,2,1024,512]{3,2,1,0:T(8,128)(2,1)}, bf16[1,2,1024,512]{3,2,1,0:T(8,128)(2,1)}, bf16[1,2,1024,512]{3,2,1,0:T(8,128)(2,1)}, f32[1024,1024]{1,0:T(8,128)}) custom-call(f32[1024,1024]{1,0:T(8,128)} %get-tuple-element.92.e_ref, bf16[8,1024,1024]{2,1,0:T(8,128)(2,1)} %get-tuple-element.93.hb_ref, f32[8,1024,4096]{2,1,0:T(8,128)} %w1_ref.33, ...), custom_call_target="tpu_custom_call" | custom-call | flops 34359738368 | bytes 67108864 | tf_op jit(solution)/shard_map/backward_layer/pallas_call | solution.py:193
  257.0 55.8 %backward_layer.9 = (bf16[2,2,1024,512]{3,2,1,0:T(8,128)(2,1)}, bf16[1,2,1024,512]{3,2,1,0:T(8,128)(2,1)}, bf16[1,2,1024,512]{3,2,1,0:T(8,128)(2,1)}, f32[1024,1024]{1,0:T(8,128)}) custom-call(f32[1024,1024]{1,0:T(8,128)} %get-tuple-element.95.e_ref, bf16[8,1024,1024]{2,1,0:T(8,128)(2,1)} %get-tuple-element.93.hb_ref, f32[8,1024,4096]{2,1,0:T(8,128)} %w1_ref.33, ...), custom_call_target="tpu_custom_call" | custom-call | flops 34359738368 | bytes 67108864 | tf_op jit(solution)/shard_map/backward_layer/pallas_call | solution.py:193
  317.9 55.0 %backward_layer.10 = (bf16[2,2,1024,512]{3,2,1,0:T(8,128)(2,1)}, bf16[1,2,1024,512]{3,2,1,0:T(8,128)(2,1)}, bf16[1,2,1024,512]{3,2,1,0:T(8,128)(2,1)}, f32[1024,1024]{1,0:T(8,128)}) custom-call(f32[1024,1024]{1,0:T(8,128)} %get-tuple-element.99.e_ref, bf16[8,1024,1024]{2,1,0:T(8,128)(2,1)} %get-tuple-element.93.hb_ref, f32[8,1024,4096]{2,1,0:T(8,128)} %w1_ref.33, ...), custom_call_target="tpu_custom_call" | custom-call | flops 34359738368 | bytes 67108864 | tf_op jit(solution)/shard_map/backward_layer/pallas_call | solution.py:193
  392.6 55.1 %backward_layer.11 = (bf16[2,2,1024,512]{3,2,1,0:T(8,128)(2,1)}, bf16[1,2,1024,512]{3,2,1,0:T(8,128)(2,1)}, bf16[1,2,1024,512]{3,2,1,0:T(8,128)(2,1)}, f32[1024,1024]{1,0:T(8,128)}) custom-call(f32[1024,1024]{1,0:T(8,128)} %get-tuple-element.105.e_ref, bf16[8,1024,1024]{2,1,0:T(8,128)(2,1)} %get-tuple-element.93.hb_ref, f32[8,1024,4096]{2,1,0:T(8,128)} %w1_ref.33, ...), custom_call_target="tpu_custom_call" | custom-call | flops 34359738368 | bytes 67108864 | tf_op jit(solution)/shard_map/backward_layer/pallas_call | solution.py:193
  459.1 55.3 %backward_layer.12 = (bf16[2,2,1024,512]{3,2,1,0:T(8,128)(2,1)}, bf16[1,2,1024,512]{3,2,1,0:T(8,128)(2,1)}, bf16[1,2,1024,512]{3,2,1,0:T(8,128)(2,1)}, f32[1024,1024]{1,0:T(8,128)}) custom-call(f32[1024,1024]{1,0:T(8,128)} %get-tuple-element.111.e_ref, bf16[8,1024,1024]{2,1,0:T(8,128)(2,1)} %get-tuple-element.93.hb_ref, f32[8,1024,4096]{2,1,0:T(8,128)} %w1_ref.33, ...), custom_call_target="tpu_custom_call" | custom-call | flops 34359738368 | bytes 67108864 | tf_op jit(solution)/shard_map/backward_layer/pallas_call | solution.py:193
  527.4 55.2 %backward_layer.13 = (bf16[2,2,1024,512]{3,2,1,0:T(8,128)(2,1)}, bf16[1,2,1024,512]{3,2,1,0:T(8,128)(2,1)}, bf16[1,2,1024,512]{3,2,1,0:T(8,128)(2,1)}, f32[1024,1024]{1,0:T(8,128)}) custom-call(f32[1024,1024]{1,0:T(8,128)} %get-tuple-element.117.e_ref, bf16[8,1024,1024]{2,1,0:T(8,128)(2,1)} %get-tuple-element.93.hb_ref, f32[8,1024,4096]{2,1,0:T(8,128)} %w1_ref.33, ...), custom_call_target="tpu_custom_call" | custom-call | flops 34359738368 | bytes 67108864 | tf_op jit(solution)/shard_map/backward_layer/pallas_call | solution.py:193
  594.8 55.4 %backward_layer.14 = (bf16[2,2,1024,512]{3,2,1,0:T(8,128)(2,1)}, bf16[1,2,1024,512]{3,2,1,0:T(8,128)(2,1)}, bf16[1,2,1024,512]{3,2,1,0:T(8,128)(2,1)}, f32[1024,1024]{1,0:T(8,128)}) custom-call(f32[1024,1024]{1,0:T(8,128)} %get-tuple-element.123.e_ref, bf16[8,1024,1024]{2,1,0:T(8,128)(2,1)} %get-tuple-element.93.hb_ref, f32[8,1024,4096]{2,1,0:T(8,128)} %w1_ref.33, ...), custom_call_target="tpu_custom_call" | custom-call | flops 34359738368 | bytes 67108864 | tf_op jit(solution)/shard_map/backward_layer/pallas_call | solution.py:193
  657.6 55.1 %backward_layer.15 = (bf16[2,2,1024,512]{3,2,1,0:T(8,128)(2,1)}, bf16[1,2,1024,512]{3,2,1,0:T(8,128)(2,1)}, bf16[1,2,1024,512]{3,2,1,0:T(8,128)(2,1)}, f32[1024,1024]{1,0:T(8,128)}) custom-call(f32[1024,1024]{1,0:T(8,128)} %get-tuple-element.129.e_ref, bf16[8,1024,1024]{2,1,0:T(8,128)(2,1)} %get-tuple-element.93.hb_ref, f32[8,1024,4096]{2,1,0:T(8,128)} %w1_ref.33, ...), custom_call_target="tpu_custom_call" | custom-call | flops 34359738368 | bytes 67108864 | tf_op jit(solution)/shard_map/backward_layer/pallas_call | solution.py:193
  718.0 43.4 %collective-permute-done.11 = bf16[2,2,1024,512]{3,2,1,0:T(8,128)(2,1)S(1)} collective-permute-done((bf16[2,2,1024,512]{3,2,1,0:T(8,128)(2,1)}, bf16[2,2,1024,512]{3,2,1,0:T(8,128)(2,1)S(1)}, u32[]{:S(2)}, u32[]{:S(2)}) %collective-permute-start.11) | collective-permute-done | bytes 4194336 | tf_op jit(solution)/shard_map/ppermute | solution.py:288
  790.7 48.8 %collective-permute-done.14 = bf16[1,2,1024,512]{3,2,1,0:T(8,128)(2,1)S(1)} collective-permute-done((bf16[1,2,1024,512]{3,2,1,0:T(8,128)(2,1)}, bf16[1,2,1024,512]{3,2,1,0:T(8,128)(2,1)S(1)}, u32[]{:S(2)}, u32[]{:S(2)}) %collective-permute-start.14) | collective-permute-done | bytes 2097184 | tf_op jit(solution)/shard_map/ppermute | solution.py:288
  845.9 59.7 %collective-permute-done.15 = bf16[1,2,1024,512]{3,2,1,0:T(8,128)(2,1)S(1)} collective-permute-done((bf16[1,2,1024,512]{3,2,1,0:T(8,128)(2,1)S(1)}, bf16[1,2,1024,512]{3,2,1,0:T(8,128)(2,1)S(1)}, u32[]{:S(2)}, u32[]{:S(2)}) %collective-permute-start.15) | collective-permute-done | bytes 2097184 | tf_op jit(solution)/shard_map/ppermute | solution.py:288
  912.7 55.4 %update_layer.8 = (f32[8,1024,4096]{2,1,0:T(8,128)}, f32[8,4096,1024]{2,1,0:T(8,128)}, f32[8,1024,4096]{2,1,0:T(8,128)}, f32[8,4096,1024]{2,1,0:T(8,128)}, f32[1024,1024]{1,0:T(8,128)}) custom-call(bf16[1024,1024]{1,0:T(8,128)(2,1)} %h_ref.1, f32[8,1024,4096]{2,1,0:T(8,128)} %w1_ref.33, f32[8,1024,4096]{2,1,0:T(8,128)} %m1_ref.15, f32[8,4096,1024]{2,1,0:T(8,128)} %w2_ref.33, ...), custom_call_target="tpu_custom_call" | custom-call | flops 17179869184 | bytes 150994944 | tf_op jit(solution)/shard_map/update_layer/pallas_call | solution.py:266
  990.3 55.0 %update_layer.9 = (f32[8,1024,4096]{2,1,0:T(8,128)}, f32[8,4096,1024]{2,1,0:T(8,128)}, f32[8,1024,4096]{2,1,0:T(8,128)}, f32[8,4096,1024]{2,1,0:T(8,128)}, f32[1024,1024]{1,0:T(8,128)}) custom-call(f32[1024,1024]{1,0:T(8,128)} %get-tuple-element.136.h_ref, ...), custom_call_target="tpu_custom_call", output_to_operand_aliasing={{0}: (6, {}), {1}: (7, {}), {2}: (8, {}), {3}: (9, {})} | custom-call | flops 17179869184 | bytes 150994944 | tf_op jit(solution)/shard_map/update_layer/pallas_call | solution.py:266
  1045.3 31.0 %all-gather.13.cloned.1.call-done.g_ref = bf16[8,2,1024,512]{3,2,1,0:T(8,128)(2,1)} async-done(((bf16[1,2,1024,512]{3,2,1,0:T(8,128)(2,1)}), bf16[8,2,1024,512]{3,2,1,0:T(8,128)(2,1)}) %all-gather.13.cloned.1.call-update) | async-done | bytes 16777232 | tf_op jit(solution)/shard_map/all_gather | solution.py:330
  1076.4 55.2 %update_layer.10 = (f32[8,1024,4096]{2,1,0:T(8,128)}, f32[8,4096,1024]{2,1,0:T(8,128)}, f32[8,1024,4096]{2,1,0:T(8,128)}, f32[8,4096,1024]{2,1,0:T(8,128)}, f32[1024,1024]{1,0:T(8,128)}) custom-call(f32[1024,1024]{1,0:T(8,128)} %get-tuple-element.142.h_ref, ...), custom_call_target="tpu_custom_call", output_to_operand_aliasing={{0}: (6, {}), {1}: (7, {}), {2}: (8, {}), {3}: (9, {})} | custom-call | flops 17179869184 | bytes 150994944 | tf_op jit(solution)/shard_map/update_layer/pallas_call | solution.py:266
  1131.6 30.7 %all-gather.15.cloned.1.call-done.g_ref = bf16[8,2,1024,512]{3,2,1,0:T(8,128)(2,1)} async-done(((bf16[1,2,1024,512]{3,2,1,0:T(8,128)(2,1)}), bf16[8,2,1024,512]{3,2,1,0:T(8,128)(2,1)}) %all-gather.15.cloned.1.call-update) | async-done | bytes 16777232 | tf_op jit(solution)/shard_map/all_gather | solution.py:330
  1162.2 55.8 %update_layer.11 = (f32[8,1024,4096]{2,1,0:T(8,128)}, f32[8,4096,1024]{2,1,0:T(8,128)}, f32[8,1024,4096]{2,1,0:T(8,128)}, f32[8,4096,1024]{2,1,0:T(8,128)}, f32[1024,1024]{1,0:T(8,128)}) custom-call(f32[1024,1024]{1,0:T(8,128)} %get-tuple-element.148.h_ref, ...), custom_call_target="tpu_custom_call", output_to_operand_aliasing={{0}: (6, {}), {1}: (7, {}), {2}: (8, {}), {3}: (9, {})} | custom-call | flops 17179869184 | bytes 150994944 | tf_op jit(solution)/shard_map/update_layer/pallas_call | solution.py:266
  1248.1 55.2 %update_layer.12 = (f32[8,1024,4096]{2,1,0:T(8,128)}, f32[8,4096,1024]{2,1,0:T(8,128)}, f32[8,1024,4096]{2,1,0:T(8,128)}, f32[8,4096,1024]{2,1,0:T(8,128)}, f32[1024,1024]{1,0:T(8,128)}) custom-call(f32[1024,1024]{1,0:T(8,128)} %get-tuple-element.153.h_ref, ...), custom_call_target="tpu_custom_call", output_to_operand_aliasing={{0}: (6, {}), {1}: (7, {}), {2}: (8, {}), {3}: (9, {})} | custom-call | flops 17179869184 | bytes 150994944 | tf_op jit(solution)/shard_map/update_layer/pallas_call | solution.py:266
  1303.3 30.7 %all-gather.19.cloned.1.call-done.g_ref = bf16[8,2,1024,512]{3,2,1,0:T(8,128)(2,1)} async-done(((bf16[1,2,1024,512]{3,2,1,0:T(8,128)(2,1)}), bf16[8,2,1024,512]{3,2,1,0:T(8,128)(2,1)}) %all-gather.19.cloned.1.call-update) | async-done | bytes 16777232 | tf_op jit(solution)/shard_map/all_gather | solution.py:330
  1334.0 55.0 %update_layer.13 = (f32[8,1024,4096]{2,1,0:T(8,128)}, f32[8,4096,1024]{2,1,0:T(8,128)}, f32[8,1024,4096]{2,1,0:T(8,128)}, f32[8,4096,1024]{2,1,0:T(8,128)}, f32[1024,1024]{1,0:T(8,128)}) custom-call(f32[1024,1024]{1,0:T(8,128)} %get-tuple-element.158.h_ref, ...), custom_call_target="tpu_custom_call", output_to_operand_aliasing={{0}: (6, {}), {1}: (7, {}), {2}: (8, {}), {3}: (9, {})} | custom-call | flops 17179869184 | bytes 150994944 | tf_op jit(solution)/shard_map/update_layer/pallas_call | solution.py:266
  1389.0 31.0 %all-gather.21.cloned.1.call-done.g_ref = bf16[8,2,1024,512]{3,2,1,0:T(8,128)(2,1)} async-done(((bf16[1,2,1024,512]{3,2,1,0:T(8,128)(2,1)}), bf16[8,2,1024,512]{3,2,1,0:T(8,128)(2,1)}) %all-gather.21.cloned.1.call-update) | async-done | bytes 16777232 | tf_op jit(solution)/shard_map/all_gather | solution.py:330
  1420.0 55.7 %update_layer.14 = (f32[8,1024,4096]{2,1,0:T(8,128)}, f32[8,4096,1024]{2,1,0:T(8,128)}, f32[8,1024,4096]{2,1,0:T(8,128)}, f32[8,4096,1024]{2,1,0:T(8,128)}, f32[1024,1024]{1,0:T(8,128)}) custom-call(f32[1024,1024]{1,0:T(8,128)} %get-tuple-element.163.h_ref, ...), custom_call_target="tpu_custom_call", output_to_operand_aliasing={{0}: (6, {}), {1}: (7, {}), {2}: (8, {}), {3}: (9, {})} | custom-call | flops 17179869184 | bytes 150994944 | tf_op jit(solution)/shard_map/update_layer/pallas_call | solution.py:266
  1506.0 53.6 %update_layer.15 = (f32[8,1024,4096]{2,1,0:T(8,128)}, f32[8,4096,1024]{2,1,0:T(8,128)}, f32[8,1024,4096]{2,1,0:T(8,128)}, f32[8,4096,1024]{2,1,0:T(8,128)}, f32[1024,1024]{1,0:T(8,128)}) custom-call(f32[1024,1024]{1,0:T(8,128)} %get-tuple-element.168.h_ref, ...), custom_call_target="tpu_custom_call", output_to_operand_aliasing={{0}: (6, {}), {1}: (7, {}), {2}: (8, {}), {3}: (9, {})} | custom-call | flops 17179869184 | bytes 150994944 | tf_op jit(solution)/shard_map/update_layer/pallas_call | solution.py:266
  (93 shorter events, 205.2 us)
Async XLA Ops:
  7.2 905.6 %all-gather.9.cloned.1.call-start = ((), (), s32[]{:S(2)}) async-start(), calls=%async_computation | async-start | bytes 18874368 | tf_op jit(solution)/shard_map/all_gather | solution.py:330
  254.5 59.8 %collective-permute-start = (bf16[2,2,1024,512]{3,2,1,0:T(8,128)(2,1)}, bf16[2,2,1024,512]{3,2,1,0:T(8,128)(2,1)}, u32[]{:S(2)}, u32[]{:S(2)}) collective-permute-start(bf16[2,2,1024,512]{3,2,1,0:T(8,128)(2,1)} %get-tuple-element.98), channel_id=1, source_target_pairs={{0,2},{1,5},{2,0},{3,7},{4,6},{5,1},{6,4},{7,3}} | collective-permute-start | bytes 12582920 | tf_op jit(solution)/shard_map/ppermute | solution.py:288
  312.8 71.3 %collective-permute-start.1 = (bf16[2,2,1024,512]{3,2,1,0:T(8,128)(2,1)}, bf16[2,2,1024,512]{3,2,1,0:T(8,128)(2,1)}, u32[]{:S(2)}, u32[]{:S(2)}) collective-permute-start(bf16[2,2,1024,512]{3,2,1,0:T(8,128)(2,1)} %get-tuple-element.102), channel_id=1, source_target_pairs={{0,2},{1,5},{2,0},{3,7},{4,6},{5,1},{6,4},{7,3}} | collective-permute-start | bytes 12582920 | tf_op jit(solution)/shard_map/ppermute | solution.py:288
  317.4 71.2 %collective-permute-start.2 = (bf16[1,2,1024,512]{3,2,1,0:T(8,128)(2,1)}, bf16[1,2,1024,512]{3,2,1,0:T(8,128)(2,1)}, u32[]{:S(2)}, u32[]{:S(2)}) collective-permute-start(bf16[1,2,1024,512]{3,2,1,0:T(8,128)(2,1)} %slice_add_fusion.15), channel_id=1, source_target_pairs={{0,4},{1,3},{2,6},{3,1},{4,0},{5,7},{6,2},{7,5}} | collective-permute-start | bytes 6291464 | tf_op jit(solution)/shard_map/ppermute | solution.py:288
  373.0 81.4 %collective-permute-start.3 = (bf16[2,2,1024,512]{3,2,1,0:T(8,128)(2,1)}, bf16[2,2,1024,512]{3,2,1,0:T(8,128)(2,1)}, u32[]{:S(2)}, u32[]{:S(2)}) collective-permute-start(bf16[2,2,1024,512]{3,2,1,0:T(8,128)(2,1)} %get-tuple-element.108), channel_id=1, source_target_pairs={{0,2},{1,5},{2,0},{3,7},{4,6},{5,1},{6,4},{7,3}} | collective-permute-start | bytes 12582920 | tf_op jit(solution)/shard_map/ppermute | solution.py:288
  387.4 61.0 %collective-permute-start.4 = (bf16[1,2,1024,512]{3,2,1,0:T(8,128)(2,1)}, bf16[1,2,1024,512]{3,2,1,0:T(8,128)(2,1)S(1)}, u32[]{:S(2)}, u32[]{:S(2)}) collective-permute-start(bf16[1,2,1024,512]{3,2,1,0:T(8,128)(2,1)} %slice_add_fusion.14), channel_id=1, source_target_pairs={{0,4},{1,3},{2,6},{3,1},{4,0},{5,7},{6,2},{7,5}} | collective-permute-start | bytes 6291464 | tf_op jit(solution)/shard_map/ppermute | solution.py:288
  447.7 71.3 %collective-permute-start.5 = (bf16[2,2,1024,512]{3,2,1,0:T(8,128)(2,1)}, bf16[2,2,1024,512]{3,2,1,0:T(8,128)(2,1)}, u32[]{:S(2)}, u32[]{:S(2)}) collective-permute-start(bf16[2,2,1024,512]{3,2,1,0:T(8,128)(2,1)} %get-tuple-element.114), channel_id=1, source_target_pairs={{0,2},{1,5},{2,0},{3,7},{4,6},{5,1},{6,4},{7,3}} | collective-permute-start | bytes 12582920 | tf_op jit(solution)/shard_map/ppermute | solution.py:288
  457.5 65.9 %collective-permute-start.6 = (bf16[1,2,1024,512]{3,2,1,0:T(8,128)(2,1)}, bf16[1,2,1024,512]{3,2,1,0:T(8,128)(2,1)}, u32[]{:S(2)}, u32[]{:S(2)}) collective-permute-start(bf16[1,2,1024,512]{3,2,1,0:T(8,128)(2,1)} %slice_add_fusion.12), channel_id=1, source_target_pairs={{0,4},{1,3},{2,6},{3,1},{4,0},{5,7},{6,2},{7,5}} | collective-permute-start | bytes 6291464 | tf_op jit(solution)/shard_map/ppermute | solution.py:288
  514.4 72.0 %collective-permute-start.7 = (bf16[2,2,1024,512]{3,2,1,0:T(8,128)(2,1)}, bf16[2,2,1024,512]{3,2,1,0:T(8,128)(2,1)}, u32[]{:S(2)}, u32[]{:S(2)}) collective-permute-start(bf16[2,2,1024,512]{3,2,1,0:T(8,128)(2,1)} %get-tuple-element.120), channel_id=1, source_target_pairs={{0,2},{1,5},{2,0},{3,7},{4,6},{5,1},{6,4},{7,3}} | collective-permute-start | bytes 12582920 | tf_op jit(solution)/shard_map/ppermute | solution.py:288
  522.3 68.6 %collective-permute-start.8 = (bf16[1,2,1024,512]{3,2,1,0:T(8,128)(2,1)}, bf16[1,2,1024,512]{3,2,1,0:T(8,128)(2,1)}, u32[]{:S(2)}, u32[]{:S(2)}) collective-permute-start(bf16[1,2,1024,512]{3,2,1,0:T(8,128)(2,1)} %slice_add_fusion.10), channel_id=1, source_target_pairs={{0,4},{1,3},{2,6},{3,1},{4,0},{5,7},{6,2},{7,5}} | collective-permute-start | bytes 6291464 | tf_op jit(solution)/shard_map/ppermute | solution.py:288
  582.6 72.5 %collective-permute-start.9 = (bf16[2,2,1024,512]{3,2,1,0:T(8,128)(2,1)}, bf16[2,2,1024,512]{3,2,1,0:T(8,128)(2,1)}, u32[]{:S(2)}, u32[]{:S(2)}) collective-permute-start(bf16[2,2,1024,512]{3,2,1,0:T(8,128)(2,1)} %get-tuple-element.126), channel_id=1, source_target_pairs={{0,2},{1,5},{2,0},{3,7},{4,6},{5,1},{6,4},{7,3}} | collective-permute-start | bytes 12582920 | tf_op jit(solution)/shard_map/ppermute | solution.py:288
  589.7 61.6 %collective-permute-start.10 = (bf16[1,2,1024,512]{3,2,1,0:T(8,128)(2,1)}, bf16[1,2,1024,512]{3,2,1,0:T(8,128)(2,1)}, u32[]{:S(2)}, u32[]{:S(2)}) collective-permute-start(bf16[1,2,1024,512]{3,2,1,0:T(8,128)(2,1)} %slice_add_fusion.8), channel_id=1, source_target_pairs={{0,4},{1,3},{2,6},{3,1},{4,0},{5,7},{6,2},{7,5}} | collective-permute-start | bytes 6291464 | tf_op jit(solution)/shard_map/ppermute | solution.py:288
  650.2 63.9 %collective-permute-start.12 = (bf16[2,2,1024,512]{3,2,1,0:T(8,128)(2,1)}, bf16[2,2,1024,512]{3,2,1,0:T(8,128)(2,1)}, u32[]{:S(2)}, u32[]{:S(2)}) collective-permute-start(bf16[2,2,1024,512]{3,2,1,0:T(8,128)(2,1)} %get-tuple-element.134), channel_id=1, source_target_pairs={{0,2},{1,5},{2,0},{3,7},{4,6},{5,1},{6,4},{7,3}} | collective-permute-start | bytes 12582920 | tf_op jit(solution)/shard_map/ppermute | solution.py:288
  712.7 48.7 %collective-permute-start.11 = (bf16[2,2,1024,512]{3,2,1,0:T(8,128)(2,1)}, bf16[2,2,1024,512]{3,2,1,0:T(8,128)(2,1)S(1)}, u32[]{:S(2)}, u32[]{:S(2)}) collective-permute-start(bf16[2,2,1024,512]{3,2,1,0:T(8,128)(2,1)} %get-tuple-element.131), channel_id=1, source_target_pairs={{0,2},{1,5},{2,0},{3,7},{4,6},{5,1},{6,4},{7,3}} | collective-permute-start | bytes 12582920 | tf_op jit(solution)/shard_map/ppermute | solution.py:288
  761.7 26.1 %collective-permute-start.13 = (bf16[1,2,1024,512]{3,2,1,0:T(8,128)(2,1)S(1)}, bf16[1,2,1024,512]{3,2,1,0:T(8,128)(2,1)S(1)}, u32[]{:S(2)}, u32[]{:S(2)}) collective-permute-start(bf16[1,2,1024,512]{3,2,1,0:T(8,128)(2,1)S(1)} %slice_add_fusion.2), channel_id=1, source_target_pairs={{0,4},{1,3},{2,6},{3,1},{4,0},{5,7},{6,2},{7,5}} | collective-permute-start | bytes 6291464 | tf_op jit(solution)/shard_map/ppermute | solution.py:288
  789.4 200.9 %all-gather.11.cloned.1.call-start = ((), (), s32[]{:S(2)}) async-start(), calls=%async_computation.1 | async-start | bytes 18874368 | tf_op jit(solution)/shard_map/all_gather | solution.py:330
  789.5 50.0 %collective-permute-start.14 = (bf16[1,2,1024,512]{3,2,1,0:T(8,128)(2,1)}, bf16[1,2,1024,512]{3,2,1,0:T(8,128)(2,1)S(1)}, u32[]{:S(2)}, u32[]{:S(2)}) collective-permute-start(bf16[1,2,1024,512]{3,2,1,0:T(8,128)(2,1)} %slice_add_fusion.3), channel_id=1, source_target_pairs={{0,4},{1,3},{2,6},{3,1},{4,0},{5,7},{6,2},{7,5}} | collective-permute-start | bytes 6291464 | tf_op jit(solution)/shard_map/ppermute | solution.py:288
  843.4 232.9 %all-gather.13.cloned.1.call-start = ((), (), s32[]{:S(2)}) async-start(), calls=%async_computation.2 | async-start | bytes 18874368 | tf_op jit(solution)/shard_map/all_gather | solution.py:330
  843.5 62.1 %collective-permute-start.15 = (bf16[1,2,1024,512]{3,2,1,0:T(8,128)(2,1)S(1)}, bf16[1,2,1024,512]{3,2,1,0:T(8,128)(2,1)S(1)}, u32[]{:S(2)}, u32[]{:S(2)}) collective-permute-start(bf16[1,2,1024,512]{3,2,1,0:T(8,128)(2,1)S(1)} %slice_add_fusion.6), channel_id=1, source_target_pairs={{0,4},{1,3},{2,6},{3,1},{4,0},{5,7},{6,2},{7,5}} | collective-permute-start | bytes 6291464 | tf_op jit(solution)/shard_map/ppermute | solution.py:288
  909.5 252.8 %all-gather.15.cloned.1.call-start = ((), (), s32[]{:S(2)}) async-start(), calls=%async_computation.3 | async-start | bytes 18874368 | tf_op jit(solution)/shard_map/all_gather | solution.py:330
  910.0 338.1 %all-gather.17.cloned.1.call-start = ((), (), s32[]{:S(2)}) async-start(), calls=%async_computation.4 | async-start | bytes 18874368 | tf_op jit(solution)/shard_map/all_gather | solution.py:330
  910.6 423.3 %all-gather.19.cloned.1.call-start = ((), (), s32[]{:S(2)}) async-start(), calls=%async_computation.5 | async-start | bytes 18874368 | tf_op jit(solution)/shard_map/all_gather | solution.py:330
  911.2 508.8 %all-gather.21.cloned.1.call-start = ((), (), s32[]{:S(2)}) async-start(), calls=%async_computation.6 | async-start | bytes 18874368 | tf_op jit(solution)/shard_map/all_gather | solution.py:330
  912.0 594.1 %all-gather.23.cloned.1.call-start = ((), (), s32[]{:S(2)}) async-start(), calls=%async_computation.7 | async-start | bytes 18874368 | tf_op jit(solution)/shard_map/all_gather | solution.py:330
  (13 other events, 489.0 us)
Sparse Core Ops, SparseCore 0:
  789.5 114.4 all-gather.8
  905.9 84.4 all-gather.10
  992.2 84.1 all-gather.12
  1078.0 84.1 all-gather.14
  1163.9 84.1 all-gather.16
  1249.8 84.1 all-gather.18
  1335.8 84.1 all-gather.20
  1421.8 84.1 all-gather.22

commit v3 on v2

--- a/solution.py
+++ b/solution.py
@@ -225,37 +225,65 @@
     )(e, hb, w_in, w_out, z)
 
 
-def update_body(step_size, first, h_ref, w1_ref, m1_ref, w2_ref, m2_ref, g_ref, *rest):
-    w1_out, w2_out, m1_out, m2_out, h_out, hb_scr = rest[0 if first else 4 :]
-    tile = g_ref.shape[-1]
-
-    @pl.when(pl.program_id(0) == 0)
+def update_body(step_size, first, parts, h_ref, w1_ref, m1_ref, w2_ref, m2_ref, *rest):
+    units, rest = rest[:parts], rest[parts + (0 if first else 4) :]
+    w1_out, w2_out, m1_out, m2_out, h_out, hb_scr, *scratch = rest
+    step = pl.program_id(0)
+    tile = w1_ref.shape[-1]
+
+    @pl.when(step == 0)
     def _():
         hb_scr[...] = h_ref[...].astype(BF)
         h_out[...] = h_ref[...].astype(F32)
 
-    m1 = MOMENTUM * m1_ref[0] + g_ref[0, 0].astype(F32)
+    if parts == 1:
+        g_ref = units[0].at[0]
+    else:
+        g_scr, sems = scratch
+        slot = lax.rem(step, 2)
+
+        def fetch(unit, at):
+            return pltpu.make_async_copy(unit.at[0], g_scr.at[at], sems.at[at])
+
+        for number, unit in enumerate(units):
+            if number == 0:
+
+                @pl.when(step == 0)
+                def _():
+                    fetch(units[0], 0).start()
+            else:
+
+                @pl.when(step == number - 1)
+                def _():
+                    fetch(unit, number % 2).start()
+
+        fetch(units[0], slot).wait()
+        g_ref = g_scr.at[slot]
+
+    m1 = MOMENTUM * m1_ref[0] + g_ref[0].astype(F32)
     m1_out[0] = m1
     w1 = w1_ref[0] - step_size * m1
     w1_out[0] = w1
     for part in range(2):
         cols = slice(part * tile, (part + 1) * tile)
-        m2 = MOMENTUM * m2_ref[0, :, cols] + g_ref[0, 1, cols, :].astype(F32)
+        m2 = MOMENTUM * m2_ref[0, :, cols] + g_ref[1, cols, :].astype(F32)
         m2_out[0, :, cols] = m2
         w2_out[0, :, cols] = w2_ref[0, :, cols] - step_size * m2
     z = dot(hb_scr[...], w1.astype(BF))
     h_out[...] += dot(gelu(z).astype(BF), w2_out[0].astype(BF))
 
 
-def update_layer(layer, h, w_in, w_out, mom_in, mom_out, grad, olds, step_size):
+def owner_tile(step):
+    return 4 * lax.rem(step, 2) + 2 * lax.div(step, 4) + lax.rem(lax.div(step, 2), 2)
+
+
+def update_layer(layer, h, w_in, w_out, mom_in, mom_out, units, olds, step_size):
     _, dim, hidden = w_in.shape
     rows = h.shape[0]
     tile = hidden // 8
     first = olds is None
-
-    def number(j):
-        return 4 * lax.rem(j, 2) + 2 * lax.div(j, 4) + lax.rem(lax.div(j, 2), 2)
-
+    parts = len(units)
+    number = owner_tile if parts == 1 else lambda j: tile_of(7 - j)
     single = pl.BlockSpec((rows, dim), lambda j: (0, 0), pipeline_mode=pl.Buffered(1))
     whole = pl.BlockSpec((rows, dim), lambda j: (0, 0))
     cols = pl.BlockSpec((1, dim, tile), lambda j: (layer, 0, number(j)))
@@ -263,29 +291,38 @@
     anyspec = pl.BlockSpec(memory_space=pl.ANY)
     shape_in = jax.ShapeDtypeStruct(w_in.shape, F32)
     shape_out = jax.ShapeDtypeStruct(w_out.shape, F32)
+    scratch = [pltpu.VMEM((rows, dim), BF)]
+    if parts == 1:
+        specs_g = [pl.BlockSpec((1, 2, dim, tile), lambda j: (j, 0, 0, 0))]
+    else:
+        specs_g = [anyspec] * parts
+        scratch += [pltpu.VMEM((2, 2, dim, tile), BF), pltpu.SemaphoreType.DMA((2,))]
     out = pl.pallas_call(
-        functools.partial(update_body, step_size, first),
+        functools.partial(update_body, step_size, first, parts),
         grid=(8,),
-        in_specs=[single, cols, cols, rws, rws, pl.BlockSpec((1, 2, dim, tile), lambda j: (j, 0, 0, 0))]
-        + ([] if first else [anyspec] * 4),
+        in_specs=[single, cols, cols, rws, rws] + specs_g + ([] if first else [anyspec] * 4),
         out_specs=[cols, rws, cols, rws, whole],
-        scratch_shapes=[pltpu.VMEM((rows, dim), BF)],
+        scratch_shapes=scratch,
         out_shape=[shape_in, shape_out, shape_in, shape_out, jax.ShapeDtypeStruct((rows, dim), F32)],
-        input_output_aliases={} if first else {6 + i: i for i in range(4)},
+        input_output_aliases={} if first else {5 + parts + i: i for i in range(4)},
         compiler_params=pltpu.CompilerParams(dimension_semantics=("arbitrary",), vmem_limit_bytes=VMEM_LIMIT),
         cost_estimate=cost(4 * rows * dim * hidden, 36 * dim * hidden),
         name="update_layer",
-    )(h, w_in, mom_in, w_out, mom_out, grad, *(() if first else olds))
+    )(h, w_in, mom_in, w_out, mom_out, *units, *(() if first else olds))
     return out[:4], out[4]
 
 
 AXES = ("y", "x", "core")
+SWAP_CORE = [(i, i ^ 1) for i in range(8)]
 SWAP_NEAR = [(i, i ^ (4 if i % 2 else 2)) for i in range(8)]
 SWAP_FAR = [(i, i ^ (2 if i % 2 else 4)) for i in range(8)]
 
 
 def swap(x, perm):
     return lax.ppermute(x, AXES, perm)
+
+
+PERMUTED = (0, 2, 4, 6)
 
 
 def after(value, *others):
@@ -322,13 +359,40 @@
                 second_exchange_sum(layer + 2)
                 err = after(err, shards[layer + 2])
         far[0] = after(far[0], far[1])
+        first_exchange_sum(0)
+        own[1] = (after(own[1][0], far[0]), *own[1][1:])
         second_exchange_sum(1)
-        first_exchange_sum(0)
         second_exchange_sum(0)
+        units = {}
+        for layer in range(layers):
+            if layer not in PERMUTED:
+                units[layer] = [lax.all_gather(shards[layer], AXES, axis=0, tiled=True)]
+
+        def spread(layer, stage, gate):
+            if layer not in PERMUTED:
+                return
+            if stage == 0:
+                mine = after(shards[layer], gate)
+                units[layer] = [mine, swap(mine, SWAP_FAR), swap(mine, SWAP_NEAR)]
+                units[layer] += [swap(mine, SWAP_CORE)]
+            elif stage == 1:
+                pair = after(units[layer][1], gate)
+                units[layer].insert(3, swap(pair, SWAP_NEAR))
+                units[layer] += [swap(pair, SWAP_CORE)]
+            else:
+                two = [after(unit, gate) for unit in units[layer][2:4]]
+                units[layer] += [swap(unit, SWAP_CORE) for unit in two]
+
         olds, h = None, x_second
+        for stage in range(3):
+            spread(0, stage, shards[0])
         for layer in range(layers):
-            grad = lax.all_gather(shards[layer], AXES, axis=0, tiled=True)
-            olds, h = update_layer(layer, h, w_in, w_out, mom_in, mom_out, grad, olds, step_size)
+            gate = h if layer else shards[0]
+            spread(layer + 2, 0, gate)
+            spread(layer + 1, 1, gate)
+            if layer:
+                spread(layer, 2, gate)
+            olds, h = update_layer(layer, h, w_in, w_out, mom_in, mom_out, units[layer], olds, step_size)
         row_diff = h - y_second.astype(F32)
         loss_rows = jnp.sum(row_diff * row_diff, axis=-1) / (2 * model_dim)
         w_in_new, w_out_new, mom_in_new, mom_out_new = olds

time: 1580 us -> 1580 us (level)
  waiting for transfers between devices: 402 us -> 382 us
  starting transfers between devices: 21.1 us -> 37.4 us
    all_gather x8 -> x4, waiting for transfers between devices: 206 us -> 0.03 us  [local_steps(): units[layer] = [lax.all_gather(shards[layer], AXES, axis=0, tiled=True)]]
    ppermute x16 -> x44, waiting for transfers between devices: 193 us -> 380 us  [swap(): return lax.ppermute(x, AXES, perm)]
    ppermute x16 -> x44, starting transfers between devices: 20.7 us -> 37.2 us  [swap(): return lax.ppermute(x, AXES, perm)]
  transfers between devices with their start and end apart: 24 -> 48, of which waited for: 14 -> 16; matrix products, arithmetic and copies ran while one was open for 3% -> 3% of each run, Pallas kernels for 49% -> 49%
where the time goes in v3:
time: 1580 us; the launch traced here: 1570 us
  Pallas kernels  1070 us (68%)
  waiting for transfers between devices  382 us (24%)
  other arithmetic  54.4 us (3%)
  starting transfers between devices  37.4 us (2%)
    pallas_call x8, Pallas kernels, backward_layer(): pl.pallas_call(backward_body, grid=(8,), in_specs=[whole, pl.BlockSpec((1...  443 us
    pallas_call x8, Pallas kernels, update_layer(): pl.pallas_call(functools.partial(update_body, step_size, first, parts), g...  440 us
    ppermute x44, waiting for transfers between devices, swap(): return lax.ppermute(x, AXES, perm)  380 us
    pallas_call x1, Pallas kernels, forward_first(): pl.pallas_call(functools.partial(forward_body, err_scale, chunk), grid=(l...  192 us
    ppermute x44, starting transfers between devices, swap(): return lax.ppermute(x, AXES, perm)  37.2 us
  transfers between devices with their start and end apart: 48, of which 16 were waited for; matrix products, arithmetic and copies ran while one was open for 3% of the time, Pallas kernels for 49%

profile of v3, /device:TPU:0, one launch (start us, length us, event | category | flops | bytes accessed | tf_op | source)
XLA Modules:
  0.0 1568.9 jit_solution(10881530205496301890)
XLA Ops:
  7.2 191.6 %forward_first.1 = (f32[8,1024,4096]{2,1,0:T(8,128)}, bf16[8,1024,1024]{2,1,0:T(8,128)(2,1)}, f32[1024,1024]{1,0:T(8,128)}) custom-call(bf16[1024,1024]{1,0:T(8,128)(2,1)} %x_ref.1, bf16[1024,1024]{1,0:T(8,128)(2,1)} %y_ref.1, f32[8,1024,4096]{2,1,0:T(8,128)} %w1_ref.33, f32[8,4096,1024]{2,1,0:T(8,128)} %w2_ref.33), custom_call_target="tpu_custom_call" | custom-call | flops 137438953472 | bytes 402653184 | tf_op jit(solution)/shard_map/forward_first/pallas_call | solution.py:70
  198.8 55.7 %backward_layer.8 = (bf16[2,2,1024,512]{3,2,1,0:T(8,128)(2,1)}, bf16[1,2,1024,512]{3,2,1,0:T(8,128)(2,1)}, bf16[1,2,1024,512]{3,2,1,0:T(8,128)(2,1)}, f32[1024,1024]{1,0:T(8,128)}) custom-call(f32[1024,1024]{1,0:T(8,128)} %get-tuple-element.109.e_ref, bf16[8,1024,1024]{2,1,0:T(8,128)(2,1)} %get-tuple-element.110.hb_ref, f32[8,1024,4096]{2,1,0:T(8,128)} %w1_ref.33, ...), custom_call_target="tpu_custom_call" | custom-call | flops 34359738368 | bytes 67108864 | tf_op jit(solution)/shard_map/backward_layer/pallas_call | solution.py:193
  257.0 55.7 %backward_layer.9 = (bf16[2,2,1024,512]{3,2,1,0:T(8,128)(2,1)}, bf16[1,2,1024,512]{3,2,1,0:T(8,128)(2,1)}, bf16[1,2,1024,512]{3,2,1,0:T(8,128)(2,1)}, f32[1024,1024]{1,0:T(8,128)}) custom-call(f32[1024,1024]{1,0:T(8,128)} %get-tuple-element.112.e_ref, bf16[8,1024,1024]{2,1,0:T(8,128)(2,1)} %get-tuple-element.110.hb_ref, f32[8,1024,4096]{2,1,0:T(8,128)} %w1_ref.33, ...), custom_call_target="tpu_custom_call" | custom-call | flops 34359738368 | bytes 67108864 | tf_op jit(solution)/shard_map/backward_layer/pallas_call | solution.py:193
  317.9 55.1 %backward_layer.10 = (bf16[2,2,1024,512]{3,2,1,0:T(8,128)(2,1)}, bf16[1,2,1024,512]{3,2,1,0:T(8,128)(2,1)}, bf16[1,2,1024,512]{3,2,1,0:T(8,128)(2,1)}, f32[1024,1024]{1,0:T(8,128)}) custom-call(f32[1024,1024]{1,0:T(8,128)} %get-tuple-element.116.e_ref, bf16[8,1024,1024]{2,1,0:T(8,128)(2,1)} %get-tuple-element.110.hb_ref, f32[8,1024,4096]{2,1,0:T(8,128)} %w1_ref.33, ...), custom_call_target="tpu_custom_call" | custom-call | flops 34359738368 | bytes 67108864 | tf_op jit(solution)/shard_map/backward_layer/pallas_call | solution.py:193
  374.2 9.8 collective-permute-done.1
  392.5 55.3 %backward_layer.11 = (bf16[2,2,1024,512]{3,2,1,0:T(8,128)(2,1)}, bf16[1,2,1024,512]{3,2,1,0:T(8,128)(2,1)}, bf16[1,2,1024,512]{3,2,1,0:T(8,128)(2,1)}, f32[1024,1024]{1,0:T(8,128)}) custom-call(f32[1024,1024]{1,0:T(8,128)} %get-tuple-element.122.e_ref, bf16[8,1024,1024]{2,1,0:T(8,128)(2,1)} %get-tuple-element.110.hb_ref, f32[8,1024,4096]{2,1,0:T(8,128)} %w1_ref.33, ...), custom_call_target="tpu_custom_call" | custom-call | flops 34359738368 | bytes 67108864 | tf_op jit(solution)/shard_map/backward_layer/pallas_call | solution.py:193
  457.3 55.2 %backward_layer.12 = (bf16[2,2,1024,512]{3,2,1,0:T(8,128)(2,1)}, bf16[1,2,1024,512]{3,2,1,0:T(8,128)(2,1)}, bf16[1,2,1024,512]{3,2,1,0:T(8,128)(2,1)}, f32[1024,1024]{1,0:T(8,128)}) custom-call(f32[1024,1024]{1,0:T(8,128)} %get-tuple-element.128.e_ref, bf16[8,1024,1024]{2,1,0:T(8,128)(2,1)} %get-tuple-element.110.hb_ref, f32[8,1024,4096]{2,1,0:T(8,128)} %w1_ref.33, ...), custom_call_target="tpu_custom_call" | custom-call | flops 34359738368 | bytes 67108864 | tf_op jit(solution)/shard_map/backward_layer/pallas_call | solution.py:193
  527.3 55.3 %backward_layer.13 = (bf16[2,2,1024,512]{3,2,1,0:T(8,128)(2,1)}, bf16[1,2,1024,512]{3,2,1,0:T(8,128)(2,1)}, bf16[1,2,1024,512]{3,2,1,0:T(8,128)(2,1)}, f32[1024,1024]{1,0:T(8,128)}) custom-call(f32[1024,1024]{1,0:T(8,128)} %get-tuple-element.134.e_ref, bf16[8,1024,1024]{2,1,0:T(8,128)(2,1)} %get-tuple-element.110.hb_ref, f32[8,1024,4096]{2,1,0:T(8,128)} %w1_ref.33, ...), custom_call_target="tpu_custom_call" | custom-call | flops 34359738368 | bytes 67108864 | tf_op jit(solution)/shard_map/backward_layer/pallas_call | solution.py:193
  594.9 55.4 %backward_layer.14 = (bf16[2,2,1024,512]{3,2,1,0:T(8,128)(2,1)}, bf16[1,2,1024,512]{3,2,1,0:T(8,128)(2,1)}, bf16[1,2,1024,512]{3,2,1,0:T(8,128)(2,1)}, f32[1024,1024]{1,0:T(8,128)}) custom-call(f32[1024,1024]{1,0:T(8,128)} %get-tuple-element.140.e_ref, bf16[8,1024,1024]{2,1,0:T(8,128)(2,1)} %get-tuple-element.110.hb_ref, f32[8,1024,4096]{2,1,0:T(8,128)} %w1_ref.33, ...), custom_call_target="tpu_custom_call" | custom-call | flops 34359738368 | bytes 67108864 | tf_op jit(solution)/shard_map/backward_layer/pallas_call | solution.py:193
  660.6 55.1 %backward_layer.15 = (bf16[2,2,1024,512]{3,2,1,0:T(8,128)(2,1)}, bf16[1,2,1024,512]{3,2,1,0:T(8,128)(2,1)}, bf16[1,2,1024,512]{3,2,1,0:T(8,128)(2,1)}, f32[1024,1024]{1,0:T(8,128)}) custom-call(f32[1024,1024]{1,0:T(8,128)} %get-tuple-element.146.e_ref, bf16[8,1024,1024]{2,1,0:T(8,128)(2,1)} %get-tuple-element.110.hb_ref, f32[8,1024,4096]{2,1,0:T(8,128)} %w1_ref.33, ...), custom_call_target="tpu_custom_call" | custom-call | flops 34359738368 | bytes 67108864 | tf_op jit(solution)/shard_map/backward_layer/pallas_call | solution.py:193
  720.0 66.9 %collective-permute-done.11 = bf16[2,2,1024,512]{3,2,1,0:T(8,128)(2,1)S(1)} collective-permute-done((bf16[2,2,1024,512]{3,2,1,0:T(8,128)(2,1)}, bf16[2,2,1024,512]{3,2,1,0:T(8,128)(2,1)S(1)}, u32[]{:S(2)}, u32[]{:S(2)}) %collective-permute-start.11) | collective-permute-done | bytes 4194336 | tf_op jit(solution)/shard_map/ppermute | solution.py:322
  795.3 51.7 %collective-permute-done.13 = bf16[1,2,1024,512]{3,2,1,0:T(8,128)(2,1)S(1)} collective-permute-done((bf16[1,2,1024,512]{3,2,1,0:T(8,128)(2,1)S(1)}, bf16[1,2,1024,512]{3,2,1,0:T(8,128)(2,1)S(1)}, u32[]{:S(2)}, u32[]{:S(2)}) %collective-permute-start.13) | collective-permute-done | bytes 2097184 | tf_op jit(solution)/shard_map/ppermute | solution.py:322
  852.4 81.2 %collective-permute-done.14.rest_1_ = bf16[1,2,1024,512]{3,2,1,0:T(8,128)(2,1)S(1)} collective-permute-done((bf16[1,2,1024,512]{3,2,1,0:T(8,128)(2,1)S(1)}, bf16[1,2,1024,512]{3,2,1,0:T(8,128)(2,1)S(1)}, u32[]{:S(2)}, u32[]{:S(2)}) %collective-permute-start.14) | collective-permute-done | bytes 2097184 | tf_op jit(solution)/shard_map/ppermute | solution.py:322
  936.5 78.7 %collective-permute-done.16.rest_3_ = bf16[1,2,1024,512]{3,2,1,0:T(8,128)(2,1)S(1)} collective-permute-done((bf16[1,2,1024,512]{3,2,1,0:T(8,128)(2,1)S(1)}, bf16[1,2,1024,512]{3,2,1,0:T(8,128)(2,1)S(1)}, u32[]{:S(2)}, u32[]{:S(2)}) %collective-permute-start.16) | collective-permute-done | bytes 2097184 | tf_op jit(solution)/shard_map/ppermute | solution.py:322
  1025.2 55.0 %update_layer.8 = (f32[8,1024,4096]{2,1,0:T(8,128)}, f32[8,4096,1024]{2,1,0:T(8,128)}, f32[8,1024,4096]{2,1,0:T(8,128)}, f32[8,4096,1024]{2,1,0:T(8,128)}, f32[1024,1024]{1,0:T(8,128)}) custom-call(bf16[1024,1024]{1,0:T(8,128)(2,1)} %h_ref.1, f32[8,1024,4096]{2,1,0:T(8,128)} %w1_ref.33, f32[8,1024,4096]{2,1,0:T(8,128)} %m1_ref.15, f32[8,4096,1024]{2,1,0:T(8,128)} %w2_ref.33, ...), custom_call_target="tpu_custom_call" | custom-call | flops 17179869184 | bytes 150994944 | tf_op jit(solution)/shard_map/update_layer/pallas_call | solution.py:300
  1082.8 55.4 %update_layer.9 = (f32[8,1024,4096]{2,1,0:T(8,128)}, f32[8,4096,1024]{2,1,0:T(8,128)}, f32[8,1024,4096]{2,1,0:T(8,128)}, f32[8,4096,1024]{2,1,0:T(8,128)}, f32[1024,1024]{1,0:T(8,128)}) custom-call(f32[1024,1024]{1,0:T(8,128)} %get-tuple-element.157.h_ref, ...), custom_call_target="tpu_custom_call", output_to_operand_aliasing={{0}: (6, {}), {1}: (7, {}), {2}: (8, {}), {3}: (9, {})} | custom-call | flops 17179869184 | bytes 150994944 | tf_op jit(solution)/shard_map/update_layer/pallas_call | solution.py:300
  1141.5 40.3 %collective-permute-done.24.rest_2_ = bf16[1,2,1024,512]{3,2,1,0:T(8,128)(2,1)} collective-permute-done((bf16[1,2,1024,512]{3,2,1,0:T(8,128)(2,1)}, bf16[1,2,1024,512]{3,2,1,0:T(8,128)(2,1)}, u32[]{:S(2)}, u32[]{:S(2)}) %collective-permute-start.24) | collective-permute-done | bytes 2097184 | tf_op jit(solution)/shard_map/ppermute | solution.py:322
  1186.2 58.8 %update_layer.10 = (f32[8,1024,4096]{2,1,0:T(8,128)}, f32[8,4096,1024]{2,1,0:T(8,128)}, f32[8,1024,4096]{2,1,0:T(8,128)}, f32[8,4096,1024]{2,1,0:T(8,128)}, f32[1024,1024]{1,0:T(8,128)}) custom-call(f32[1024,1024]{1,0:T(8,128)} %get-tuple-element.164.h_ref, ...), custom_call_target="tpu_custom_call", output_to_operand_aliasing={{0}: (13, {}), {1}: (14, {}), {2}: (15, {}), {3}: (16, {})} | custom-call | flops 17179869184 | bytes 150994944 | tf_op jit(solution)/shard_map/update_layer/pallas_call | solution.py:300
  1245.1 25.2 %collective-permute-done.30.rest_1_ = bf16[1,2,1024,512]{3,2,1,0:T(8,128)(2,1)} collective-permute-done((bf16[1,2,1024,512]{3,2,1,0:T(8,128)(2,1)}, bf16[1,2,1024,512]{3,2,1,0:T(8,128)(2,1)}, u32[]{:S(2)}, u32[]{:S(2)}) %collective-permute-start.30) | collective-permute-done | bytes 2097184 | tf_op jit(solution)/shard_map/ppermute | solution.py:322
  1272.7 54.5 %update_layer.11 = (f32[8,1024,4096]{2,1,0:T(8,128)}, f32[8,4096,1024]{2,1,0:T(8,128)}, f32[8,1024,4096]{2,1,0:T(8,128)}, f32[8,4096,1024]{2,1,0:T(8,128)}, f32[1024,1024]{1,0:T(8,128)}) custom-call(f32[1024,1024]{1,0:T(8,128)} %get-tuple-element.174.h_ref, ...), custom_call_target="tpu_custom_call", output_to_operand_aliasing={{0}: (6, {}), {1}: (7, {}), {2}: (8, {}), {3}: (9, {})} | custom-call | flops 17179869184 | bytes 150994944 | tf_op jit(solution)/shard_map/update_layer/pallas_call | solution.py:300
  1334.8 54.3 %update_layer.12 = (f32[8,1024,4096]{2,1,0:T(8,128)}, f32[8,4096,1024]{2,1,0:T(8,128)}, f32[8,1024,4096]{2,1,0:T(8,128)}, f32[8,4096,1024]{2,1,0:T(8,128)}, f32[1024,1024]{1,0:T(8,128)}) custom-call(f32[1024,1024]{1,0:T(8,128)} %get-tuple-element.179.h_ref, ...), custom_call_target="tpu_custom_call", output_to_operand_aliasing={{0}: (13, {}), {1}: (14, {}), {2}: (15, {}), {3}: (16, {})} | custom-call | flops 17179869184 | bytes 150994944 | tf_op jit(solution)/shard_map/update_layer/pallas_call | solution.py:300
  1389.6 53.5 %update_layer.13 = (f32[8,1024,4096]{2,1,0:T(8,128)}, f32[8,4096,1024]{2,1,0:T(8,128)}, f32[8,1024,4096]{2,1,0:T(8,128)}, f32[8,4096,1024]{2,1,0:T(8,128)}, f32[1024,1024]{1,0:T(8,128)}) custom-call(f32[1024,1024]{1,0:T(8,128)} %get-tuple-element.188.h_ref, ...), custom_call_target="tpu_custom_call", output_to_operand_aliasing={{0}: (6, {}), {1}: (7, {}), {2}: (8, {}), {3}: (9, {})} | custom-call | flops 17179869184 | bytes 150994944 | tf_op jit(solution)/shard_map/update_layer/pallas_call | solution.py:300
  1450.6 54.4 %update_layer.14 = (f32[8,1024,4096]{2,1,0:T(8,128)}, f32[8,4096,1024]{2,1,0:T(8,128)}, f32[8,1024,4096]{2,1,0:T(8,128)}, f32[8,4096,1024]{2,1,0:T(8,128)}, f32[1024,1024]{1,0:T(8,128)}) custom-call(f32[1024,1024]{1,0:T(8,128)} %get-tuple-element.193.h_ref, ...), custom_call_target="tpu_custom_call", output_to_operand_aliasing={{0}: (13, {}), {1}: (14, {}), {2}: (15, {}), {3}: (16, {})} | custom-call | flops 17179869184 | bytes 150994944 | tf_op jit(solution)/shard_map/update_layer/pallas_call | solution.py:300
  1505.1 53.7 %update_layer.15 = (f32[8,1024,4096]{2,1,0:T(8,128)}, f32[8,4096,1024]{2,1,0:T(8,128)}, f32[8,1024,4096]{2,1,0:T(8,128)}, f32[8,4096,1024]{2,1,0:T(8,128)}, f32[1024,1024]{1,0:T(8,128)}) custom-call(f32[1024,1024]{1,0:T(8,128)} %get-tuple-element.202.h_ref, ...), custom_call_target="tpu_custom_call", output_to_operand_aliasing={{0}: (6, {}), {1}: (7, {}), {2}: (8, {}), {3}: (9, {})} | custom-call | flops 17179869184 | bytes 150994944 | tf_op jit(solution)/shard_map/update_layer/pallas_call | solution.py:300
  (167 shorter events, 126.9 us)
Async XLA Ops:
  7.2 1075.6 %all-gather.5.cloned.1.call-start = ((), (), s32[]{:S(2)}) async-start(), calls=%async_computation | async-start | bytes 18874368 | tf_op jit(solution)/shard_map/all_gather | solution.py:369
  312.7 71.3 %collective-permute-start.1 = (bf16[2,2,1024,512]{3,2,1,0:T(8,128)(2,1)}, bf16[2,2,1024,512]{3,2,1,0:T(8,128)(2,1)}, u32[]{:S(2)}, u32[]{:S(2)}) collective-permute-start(bf16[2,2,1024,512]{3,2,1,0:T(8,128)(2,1)} %get-tuple-element.119), channel_id=1, source_target_pairs={{0,2},{1,5},{2,0},{3,7},{4,6},{5,1},{6,4},{7,3}} | collective-permute-start | bytes 12582920 | tf_op jit(solution)/shard_map/ppermute | solution.py:322
  317.3 71.2 %collective-permute-start.2 = (bf16[1,2,1024,512]{3,2,1,0:T(8,128)(2,1)}, bf16[1,2,1024,512]{3,2,1,0:T(8,128)(2,1)}, u32[]{:S(2)}, u32[]{:S(2)}) collective-permute-start(bf16[1,2,1024,512]{3,2,1,0:T(8,128)(2,1)} %slice_add_fusion.15), channel_id=1, source_target_pairs={{0,4},{1,3},{2,6},{3,1},{4,0},{5,7},{6,2},{7,5}} | collective-permute-start | bytes 6291464 | tf_op jit(solution)/shard_map/ppermute | solution.py:322
  372.9 79.7 %collective-permute-start.3 = (bf16[2,2,1024,512]{3,2,1,0:T(8,128)(2,1)}, bf16[2,2,1024,512]{3,2,1,0:T(8,128)(2,1)}, u32[]{:S(2)}, u32[]{:S(2)}) collective-permute-start(bf16[2,2,1024,512]{3,2,1,0:T(8,128)(2,1)} %get-tuple-element.125), channel_id=1, source_target_pairs={{0,2},{1,5},{2,0},{3,7},{4,6},{5,1},{6,4},{7,3}} | collective-permute-start | bytes 12582920 | tf_op jit(solution)/shard_map/ppermute | solution.py:322
  447.8 71.3 %collective-permute-start.5 = (bf16[2,2,1024,512]{3,2,1,0:T(8,128)(2,1)}, bf16[2,2,1024,512]{3,2,1,0:T(8,128)(2,1)}, u32[]{:S(2)}, u32[]{:S(2)}) collective-permute-start(bf16[2,2,1024,512]{3,2,1,0:T(8,128)(2,1)} %get-tuple-element.131), channel_id=1, source_target_pairs={{0,2},{1,5},{2,0},{3,7},{4,6},{5,1},{6,4},{7,3}} | collective-permute-start | bytes 12582920 | tf_op jit(solution)/shard_map/ppermute | solution.py:322
  512.4 74.1 %collective-permute-start.7 = (bf16[2,2,1024,512]{3,2,1,0:T(8,128)(2,1)}, bf16[2,2,1024,512]{3,2,1,0:T(8,128)(2,1)}, u32[]{:S(2)}, u32[]{:S(2)}) collective-permute-start(bf16[2,2,1024,512]{3,2,1,0:T(8,128)(2,1)} %get-tuple-element.137), channel_id=1, source_target_pairs={{0,2},{1,5},{2,0},{3,7},{4,6},{5,1},{6,4},{7,3}} | collective-permute-start | bytes 12582920 | tf_op jit(solution)/shard_map/ppermute | solution.py:322
  582.6 74.9 %collective-permute-start.9 = (bf16[2,2,1024,512]{3,2,1,0:T(8,128)(2,1)}, bf16[2,2,1024,512]{3,2,1,0:T(8,128)(2,1)}, u32[]{:S(2)}, u32[]{:S(2)}) collective-permute-start(bf16[2,2,1024,512]{3,2,1,0:T(8,128)(2,1)} %get-tuple-element.143), channel_id=1, source_target_pairs={{0,2},{1,5},{2,0},{3,7},{4,6},{5,1},{6,4},{7,3}} | collective-permute-start | bytes 12582920 | tf_op jit(solution)/shard_map/ppermute | solution.py:322
  715.7 71.2 %collective-permute-start.11 = (bf16[2,2,1024,512]{3,2,1,0:T(8,128)(2,1)}, bf16[2,2,1024,512]{3,2,1,0:T(8,128)(2,1)S(1)}, u32[]{:S(2)}, u32[]{:S(2)}) collective-permute-start(bf16[2,2,1024,512]{3,2,1,0:T(8,128)(2,1)} %get-tuple-element.148), channel_id=1, source_target_pairs={{0,2},{1,5},{2,0},{3,7},{4,6},{5,1},{6,4},{7,3}} | collective-permute-start | bytes 12582920 | tf_op jit(solution)/shard_map/ppermute | solution.py:322
  792.2 480.5 %all-gather.7.cloned.1.call-start = ((), (), s32[]{:S(2)}) async-start(), calls=%async_computation.1 | async-start | bytes 18874368 | tf_op jit(solution)/shard_map/all_gather | solution.py:369
  793.0 596.6 %all-gather.9.cloned.1.call-start = ((), (), s32[]{:S(2)}) async-start(), calls=%async_computation.2 | async-start | bytes 18874368 | tf_op jit(solution)/shard_map/all_gather | solution.py:369
  793.7 711.4 %all-gather.11.cloned.1.call-start = ((), (), s32[]{:S(2)}) async-start(), calls=%async_computation.3 | async-start | bytes 18874368 | tf_op jit(solution)/shard_map/all_gather | solution.py:369
  849.7 84.0 %collective-permute-start.14 = (bf16[1,2,1024,512]{3,2,1,0:T(8,128)(2,1)S(1)}, bf16[1,2,1024,512]{3,2,1,0:T(8,128)(2,1)S(1)}, u32[]{:S(2)}, u32[]{:S(2)}) collective-permute-start(bf16[1,2,1024,512]{3,2,1,0:T(8,128)(2,1)S(1)} %fusion.2.rest_0_), channel_id=1, source_target_pairs={{0,4},{1,3},{2,6},{3,1},{4,0},{5,7},{6,2},{7,5}} | collective-permute-start | bytes 6291464 | tf_op jit(solution)/shard_map/ppermute | solution.py:322
  852.3 84.2 %collective-permute-start.15 = (bf16[1,2,1024,512]{3,2,1,0:T(8,128)(2,1)S(1)}, bf16[1,2,1024,512]{3,2,1,0:T(8,128)(2,1)S(1)}, u32[]{:S(2)}, u32[]{:S(2)}) collective-permute-start(bf16[1,2,1024,512]{3,2,1,0:T(8,128)(2,1)S(1)} %fusion.2.rest_0_), channel_id=1, source_target_pairs={{0,2},{1,5},{2,0},{3,7},{4,6},{5,1},{6,4},{7,3}} | collective-permute-start | bytes 6291464 | tf_op jit(solution)/shard_map/ppermute | solution.py:322
  933.7 81.6 %collective-permute-start.16 = (bf16[1,2,1024,512]{3,2,1,0:T(8,128)(2,1)S(1)}, bf16[1,2,1024,512]{3,2,1,0:T(8,128)(2,1)S(1)}, u32[]{:S(2)}, u32[]{:S(2)}) collective-permute-start(bf16[1,2,1024,512]{3,2,1,0:T(8,128)(2,1)S(1)} %collective-permute-done.14.rest_1_), channel_id=1, source_target_pairs={{0,2},{1,5},{2,0},{3,7},{4,6},{5,1},{6,4},{7,3}} | collective-permute-start | bytes 6291464 | tf_op jit(solution)/shard_map/ppermute | solution.py:322
  934.8 81.8 %collective-permute-start.22 = (bf16[1,2,1024,512]{3,2,1,0:T(8,128)(2,1)S(1)}, bf16[1,2,1024,512]{3,2,1,0:T(8,128)(2,1)S(1)}, u32[]{:S(2)}, u32[]{:S(2)}) collective-permute-start(bf16[1,2,1024,512]{3,2,1,0:T(8,128)(2,1)S(1)} %copy-done.11), channel_id=1, source_target_pairs={{0,4},{1,3},{2,6},{3,1},{4,0},{5,7},{6,2},{7,5}} | collective-permute-start | bytes 6291464 | tf_op jit(solution)/shard_map/ppermute | solution.py:322
  936.0 85.8 %collective-permute-start.17 = (bf16[1,2,1024,512]{3,2,1,0:T(8,128)(2,1)S(1)}, bf16[1,2,1024,512]{3,2,1,0:T(8,128)(2,1)S(1)}, u32[]{:S(2)}, u32[]{:S(2)}) collective-permute-start(bf16[1,2,1024,512]{3,2,1,0:T(8,128)(2,1)S(1)} %fusion.2.rest_0_), channel_id=1, source_target_pairs={{0,1},{1,0},{2,3},{3,2},{4,5},{5,4},{6,7},{7,6}} | collective-permute-start | bytes 6291464 | tf_op jit(solution)/shard_map/ppermute | solution.py:322
  936.0 85.8 %collective-permute-start.18 = (bf16[1,2,1024,512]{3,2,1,0:T(8,128)(2,1)S(1)}, bf16[1,2,1024,512]{3,2,1,0:T(8,128)(2,1)S(1)}, u32[]{:S(2)}, u32[]{:S(2)}) collective-permute-start(bf16[1,2,1024,512]{3,2,1,0:T(8,128)(2,1)S(1)} %collective-permute-done.14.rest_1_), channel_id=1, source_target_pairs={{0,1},{1,0},{2,3},{3,2},{4,5},{5,4},{6,7},{7,6}} | collective-permute-start | bytes 6291464 | tf_op jit(solution)/shard_map/ppermute | solution.py:322
  936.5 85.3 %collective-permute-start.19 = (bf16[1,2,1024,512]{3,2,1,0:T(8,128)(2,1)S(1)}, bf16[1,2,1024,512]{3,2,1,0:T(8,128)(2,1)S(1)}, u32[]{:S(2)}, u32[]{:S(2)}) collective-permute-start(bf16[1,2,1024,512]{3,2,1,0:T(8,128)(2,1)S(1)} %collective-permute-done.15.rest_2_), channel_id=1, source_target_pairs={{0,1},{1,0},{2,3},{3,2},{4,5},{5,4},{6,7},{7,6}} | collective-permute-start | bytes 6291464 | tf_op jit(solution)/shard_map/ppermute | solution.py:322
  1081.5 100.3 %collective-permute-start.24 = (bf16[1,2,1024,512]{3,2,1,0:T(8,128)(2,1)}, bf16[1,2,1024,512]{3,2,1,0:T(8,128)(2,1)}, u32[]{:S(2)}, u32[]{:S(2)}) collective-permute-start(bf16[1,2,1024,512]{3,2,1,0:T(8,128)(2,1)} %fusion.rest_0_), channel_id=1, source_target_pairs={{0,2},{1,5},{2,0},{3,7},{4,6},{5,1},{6,4},{7,3}} | collective-permute-start | bytes 6291464 | tf_op jit(solution)/shard_map/ppermute | solution.py:322
  1082.3 100.9 %collective-permute-start.26 = (bf16[1,2,1024,512]{3,2,1,0:T(8,128)(2,1)}, bf16[1,2,1024,512]{3,2,1,0:T(8,128)(2,1)}, u32[]{:S(2)}, u32[]{:S(2)}) collective-permute-start(bf16[1,2,1024,512]{3,2,1,0:T(8,128)(2,1)} %fusion.rest_0_), channel_id=1, source_target_pairs={{0,1},{1,0},{2,3},{3,2},{4,5},{5,4},{6,7},{7,6}} | collective-permute-start | bytes 6291464 | tf_op jit(solution)/shard_map/ppermute | solution.py:322
  1082.3 101.8 %collective-permute-start.27 = (bf16[1,2,1024,512]{3,2,1,0:T(8,128)(2,1)}, bf16[1,2,1024,512]{3,2,1,0:T(8,128)(2,1)}, u32[]{:S(2)}, u32[]{:S(2)}) collective-permute-start(bf16[1,2,1024,512]{3,2,1,0:T(8,128)(2,1)} %collective-permute-done.23.rest_1_), channel_id=1, source_target_pairs={{0,1},{1,0},{2,3},{3,2},{4,5},{5,4},{6,7},{7,6}} | collective-permute-start | bytes 6291464 | tf_op jit(solution)/shard_map/ppermute | solution.py:322
  1182.1 88.2 %collective-permute-start.30 = (bf16[1,2,1024,512]{3,2,1,0:T(8,128)(2,1)}, bf16[1,2,1024,512]{3,2,1,0:T(8,128)(2,1)}, u32[]{:S(2)}, u32[]{:S(2)}) collective-permute-start(bf16[1,2,1024,512]{3,2,1,0:T(8,128)(2,1)} %fusion.4.rest_0_), channel_id=1, source_target_pairs={{0,4},{1,3},{2,6},{3,1},{4,0},{5,7},{6,2},{7,5}} | collective-permute-start | bytes 6291464 | tf_op jit(solution)/shard_map/ppermute | solution.py:322
  1183.2 144.0 %collective-permute-start.31 = (bf16[1,2,1024,512]{3,2,1,0:T(8,128)(2,1)}, bf16[1,2,1024,512]{3,2,1,0:T(8,128)(2,1)}, u32[]{:S(2)}, u32[]{:S(2)}) collective-permute-start(bf16[1,2,1024,512]{3,2,1,0:T(8,128)(2,1)} %fusion.4.rest_0_), channel_id=1, source_target_pairs={{0,2},{1,5},{2,0},{3,7},{4,6},{5,1},{6,4},{7,3}} | collective-permute-start | bytes 6291464 | tf_op jit(solution)/shard_map/ppermute | solution.py:322
  1327.8 115.3 %collective-permute-start.38 = (bf16[1,2,1024,512]{3,2,1,0:T(8,128)(2,1)}, bf16[1,2,1024,512]{3,2,1,0:T(8,128)(2,1)}, u32[]{:S(2)}, u32[]{:S(2)}) collective-permute-start(bf16[1,2,1024,512]{3,2,1,0:T(8,128)(2,1)} %fusion.6.rest_0_), channel_id=1, source_target_pairs={{0,2},{1,5},{2,0},{3,7},{4,6},{5,1},{6,4},{7,3}} | collective-permute-start | bytes 6291464 | tf_op jit(solution)/shard_map/ppermute | solution.py:322
  (52 other events, 2300.7 us)
Sparse Core Ops, SparseCore 0:
  792.3 134.3 all-gather.4
  928.6 129.5 all-gather.6
  1060.0 111.8 all-gather.8
  1173.6 136.3 all-gather.10
